TPU v7x, 256 devices: a whole 4x4x8 slice. The times are simulated.
256 devices in a mesh: row: 8 (over y_lo, x), col: 32 (over z, y_hi, core).
Axes of the slice: x: 4, y: 4 (y_hi: 2, y_lo: 2; y = y_hi * 2 + y_lo), z: 8, core: 2. Of those that a mesh axis runs over, the one named last changes fastest.
Arguments:
- charge: float32 [256, 256, 256], P('col', 'row'), may hold values from -6 to 6
- green_spectrum: float32 [512, 512, 512], P('row', 'col'), may hold values from 0.2 to 2
Outputs:
- potential: float32 [256, 256, 256], P('col', 'row')
All inputs are finite; a program needn't handle non-finite values.
Results may differ from a plain program's by a relative error of at most 0.00007.
Values sent between devices are 32-bit elements; how exact they have to be, the bound alone decides.
No kernel may reach another device: no remote copies, remote signals or barrier semaphores. Data moves between devices by JAX's collectives and lax.ppermute only.
A program may use at most 128 MiB of HBM per device.

v0:
```python
import math

import jax
import jax.numpy as jnp
from jax import lax
from jax.sharding import PartitionSpec as P

M = 512
N = 256


def in_blocks(value, dim, devices):
    lengths = value.shape
    parts = value.reshape(*lengths[:dim], devices, lengths[dim] // devices, *lengths[dim + 1 :])
    return jnp.moveaxis(parts, dim, 0)


def piece_ends(length, count):
    unit = 8 if length >= 8 * count else 1
    return [length // unit * k // count * unit for k in range(1, count)]


def in_order(parts, dim):
    parts = jnp.moveaxis(parts, 0, dim)
    lengths = parts.shape
    return parts.reshape(*lengths[:dim], lengths[dim] * lengths[dim + 1], *lengths[dim + 2 :])


def exchange_in_pieces(value, axis, pieces, split_dim, concat_dim):
    parts = in_blocks(value, split_dim, lax.axis_size(axis))
    cut = max(range(1, max(2, parts.ndim - 1)), key=lambda d: parts.shape[d])
    done = []
    for piece in jnp.split(parts, piece_ends(parts.shape[cut], pieces), axis=cut):
        if piece.size:
            done.append(lax.all_to_all(piece, axis, split_axis=0, concat_axis=0, tiled=True))
    return in_order(jnp.concatenate(done, axis=cut), concat_dim)


def phases(count_in, count_out, length):
    row_ids = lax.iota(jnp.int32, count_in)[:, None]
    col_ids = lax.iota(jnp.int32, count_out)[None, :]
    turn_ids = row_ids * col_ids % length
    angles = turn_ids.astype(jnp.float32) * (2.0 * math.pi / length)
    return (jnp.cos(angles), jnp.sin(angles))


def forward_table(count_in, count_out, length):
    cosine, sine_part = phases(count_in, count_out, length)
    return jnp.stack([jnp.stack([cosine, -sine_part], 1), jnp.stack([sine_part, cosine], 1)], 0)


def inverse_table(count_in, count_out, length):
    cosine, sine_part = phases(count_in, count_out, length)
    scaling = 1.0 / length
    return (
        jnp.stack([jnp.stack([cosine, sine_part], 1), jnp.stack([-sine_part, cosine], 1)], 0)
        * scaling
    )


def contract(pattern, left_side, right_side):
    return jnp.einsum(
        pattern,
        left_side,
        right_side,
        precision=lax.Precision.HIGHEST,
        preferred_element_type=jnp.float32,
    )


def on_device(charge, green_spectrum):
    cosine, sine_part = phases(N, M, M)
    real_table = jnp.stack([cosine, -sine_part], 1)
    along_z = contract("xyz,zqk->xyqk", charge, real_table)
    by_rows = exchange_in_pieces(along_z, "row", 2, 3, 1)
    forward = forward_table(N, M, M)
    along_y = contract("xypk,pyqb->xkqb", by_rows, forward)
    spectrum = contract(
        "xkpj,pxqa->kjqa",
        lax.all_to_all(along_y, "col", split_axis=3, concat_axis=0, tiled=True),
        forward,
    )
    product = spectrum * green_spectrum[:, :, None, :]
    back_table = inverse_table(M, N, M)
    back_cos, back_sin = phases(M, N, M)
    real_back = jnp.stack([back_cos, -back_sin], 0) * (1.0 / M)
    back_x = contract("kjqa,qapx->kjpx", product, back_table)
    by_cols = lax.all_to_all(back_x, "col", split_axis=3, concat_axis=1, tiled=True)
    back_y = contract("kbpx,pbqy->kxqy", by_cols, back_table)
    return contract(
        "cxpy,pcz->xyz",
        lax.all_to_all(back_y, "row", split_axis=3, concat_axis=0, tiled=True),
        real_back,
    )


def solution(mesh):
    in_specs = (P("col", "row", None), P("row", "col", None))
    out_specs = P("col", "row", None)
    return jax.shard_map(
        on_device, mesh=mesh, in_specs=in_specs, out_specs=out_specs, check_vma=False
    )
```

profile of v0, /device:TPU:1, one launch (start us, length us, event | category | flops | bytes accessed | tf_op | source)
XLA Modules:
  0.0 302.0 jit_solution(13520128151849072066)
XLA Ops:
  0.0 0.0 copy-start
  0.0 2.1 fusion.54
  2.1 0.0 copy-start.3
  2.1 0.0 copy-start.5
  2.1 0.8 copy-done.3
  2.9 0.2 copy-done.5
  3.1 0.0 copy-done
  3.1 1.1 convolution_bitcast_fusion
  4.2 0.4 reshape.228
  4.6 0.4 copy.82
  5.0 0.3 fusion.64
  5.3 1.4 reshape.245
  6.7 6.0 %all-to-all-start.1 = ((f32[8,1,16384]{2,1,0:T(1,128)}), f32[8,1,16384]{2,1,0:T(1,128)S(1)}, u32[]{:S(2)}, u32[]{:S(2)}) async-start(f32[8,1,16384]{2,1,0:T(1,128)} %reshape.245), calls=%async_computation.1 | async-start | bytes 1048576 | tf_op jit(solution)/shard_map/all_to_all | solution.py:35
  12.7 1.4 reshape.247
  14.2 8.8 %all-to-all-done.1 = f32[8,1,16384]{2,1,0:T(1,128)S(1)} async-done(((f32[8,1,16384]{2,1,0:T(1,128)}), f32[8,1,16384]{2,1,0:T(1,128)S(1)}, u32[]{:S(2)}, u32[]{:S(2)}) %all-to-all-start.1) | async-done | bytes 524320 | tf_op jit(solution)/shard_map/all_to_all | solution.py:35
  23.0 4.3 %all-to-all-start = ((f32[8,1,16384]{2,1,0:T(1,128)}), f32[8,1,16384]{2,1,0:T(1,128)}, u32[]{:S(2)}, u32[]{:S(2)}) async-start(f32[8,1,16384]{2,1,0:T(1,128)} %reshape.247), calls=%async_computation | async-start | bytes 1048576 | tf_op jit(solution)/shard_map/all_to_all | solution.py:35
  27.3 0.0 copy-done.8
  27.3 1.9 fusion.53
  29.2 0.0 copy-done.4
  29.2 0.0 copy-done.6
  29.2 0.3 fusion.29
  29.5 0.5 broadcast.343
  30.1 3.8 %reduce = f32[8,16384]{1,0:T(8,128)} reduce(f32[8,1,16384]{2,1,0:T(1,128)} %copy-done.8, f32[]{:T(128)} %broadcast.343), dimensions={1}, to_apply=%all_to_all.46.reduce_sub_computation | reduce | bytes 1048580 | tf_op jit(solution)/shard_map/all_to_all | solution.py:35
  33.9 1.5 reshape.246
  35.3 2.3 all-to-all-done
  37.6 3.8 %reduce.1 = f32[8,16384]{1,0:T(8,128)} reduce(f32[8,1,16384]{2,1,0:T(1,128)} %all-to-all-done, f32[]{:T(128)} %broadcast.343), dimensions={1}, to_apply=%all_to_all.45.reduce_sub_computation | reduce | bytes 1048580 | tf_op jit(solution)/shard_map/all_to_all | solution.py:35
  41.4 2.4 reshape.248
  43.8 1.5 maximum_bitcast_fusion
  45.3 0.2 copy.37
  45.6 5.2 %fusion.10 = f32[8,64,2,512]{3,1,2,0:T(8,128)} fusion(f32[8,256,2,64,1]{3,1,2,4,0:T(8,128)S(1)} %bitcast.118, f32[1,256,2,512]{3,1,2,0:T(8,128)S(1)} %get-tuple-element.10, f32[1,256,2,512]{3,1,2,0:T(8,128)S(1)} %get-tuple-element.9), kind=kOutput, calls=%fused_computation.15 | convolution fusion | flops 3221749760 | bytes 5242880 | tf_op jit(solution)/shard_map/xypk,pyqb->xkqb/dot_general | solution.py:62
  50.7 6.7 %copy.40 = f32[8,64,2,512]{1,2,0,3:T(2,128)} copy(f32[8,64,2,512]{3,1,2,0:T(8,128)} %fusion.10) | data formatting | bytes 4194304 | tf_op jit(solution)/shard_map/xypk,pyqb->xkqb/dot_general | solution.py:62
  57.4 6.6 %reshape.249 = f32[32,1,16384]{2,1,0:T(1,128)} reshape(f32[512,8,2,64]{3,2,1,0:T(2,128)} %bitcast.111) | data formatting | bytes 4194304
  64.0 11.8 %all-to-all-start.2 = ((f32[32,1,16384]{2,1,0:T(1,128)}), f32[32,1,16384]{2,1,0:T(1,128)}, u32[]{:S(2)}, u32[]{:S(2)}) async-start(f32[32,1,16384]{2,1,0:T(1,128)} %reshape.249), calls=%async_computation.2 | async-start | bytes 4194304 | tf_op jit(solution)/shard_map/all_to_all | solution.py:80
  75.7 1.9 fusion.56
  77.7 2.1 fusion.51
  79.7 0.2 maximum_bitcast_fusion.2
  79.9 45.9 %all-to-all-done.2 = f32[32,1,16384]{2,1,0:T(1,128)} async-done(((f32[32,1,16384]{2,1,0:T(1,128)}), f32[32,1,16384]{2,1,0:T(1,128)}, u32[]{:S(2)}, u32[]{:S(2)}) %all-to-all-start.2) | async-done | bytes 2097184 | tf_op jit(solution)/shard_map/all_to_all | solution.py:80
  125.8 8.7 %reduce.2 = f32[32,16384]{1,0:T(8,128)} reduce(f32[32,1,16384]{2,1,0:T(1,128)} %all-to-all-done.2, f32[]{:T(128)} %broadcast.343), dimensions={1}, to_apply=%all_to_all.47.reduce_sub_computation | reduce | bytes 4194308 | tf_op jit(solution)/shard_map/all_to_all | solution.py:80
  134.6 5.6 %reshape.250 = f32[512,8,2,64]{3,2,1,0:T(2,128)} reshape(f32[32,16384]{1,0:T(8,128)} %reduce.2) | data formatting | bytes 4194304
  140.2 3.5 %copy.41 = f32[8,64,2,512]{1,3,2,0:T(8,128)S(1)} copy(f32[8,64,2,512]{1,2,0,3:T(2,128)} %bitcast.113) | data formatting | bytes 4194304 | tf_op jit(solution)/shard_map/all_to_all | solution.py:80
  143.7 2.6 copy.42
  146.3 5.4 %copy.56 = f32[256,64,2,16,1]{0,3,2,4,1:T(8,128)} copy(f32[256,64,2,16,1]{1,3,2,0,4:T(8,128)} %bitcast.115) | data formatting | bytes 4194304 | tf_op jit(solution)/shard_map/all_to_all | solution.py:80
  151.7 0.0 copy-start.7
  151.7 9.3 %fusion.3 = f32[64,16,2,512,1]{3,1,4,2,0:T(8,128)S(1)} fusion(f32[256,64,2,16,1]{0,3,2,4,1:T(8,128)} %copy.56, f32[1,256,2,512]{3,1,2,0:T(8,128)} %copy-done.2, f32[1,256,2,512]{3,1,2,0:T(8,128)S(1)} %get-tuple-element.9), kind=kOutput, calls=%fused_computation.7 | convolution fusion | flops 6442975232 | bytes 8388608 | tf_op jit(solution)/shard_map/xkpj,pxqa->kjqa/dot_general | solution.py:62
  161.0 8.5 %fusion.13 = f32[64,16,2,256]{3,1,2,0:T(8,128)} fusion(f32[64,16,2,512,1]{3,1,4,2,0:T(8,128)S(1)} %fusion.3, f32[64,16,512]{2,1,0:T(8,128)S(1)} %copy-done.7, f32[1,512,2,256]{3,1,0,2:T(8,128)S(1)} %get-tuple-element.8, f32[1,512,2,256]{3,1,0,2:T(8,128)S(1)} %get-tuple-element.7), kind=kOutput, calls=%fused_computation.16 | convolution fusion | flops 6444548096 | bytes 10485760 | tf_op jit(solution)/shard_map/kjqa,qapx->kjpx/dot_general | solution.py:62
  169.6 5.6 %copy.46 = f32[64,16,2,256]{0,1,2,3:T(8,128)} copy(f32[64,16,2,256]{3,1,2,0:T(8,128)} %fusion.13) | data formatting | bytes 4194304 | tf_op jit(solution)/shard_map/kjqa,qapx->kjpx/dot_general | solution.py:62
  175.1 5.4 %reshape.251 = f32[32,1,16384]{2,1,0:T(1,128)} reshape(f32[256,2,16,64]{3,2,1,0:T(8,128)} %bitcast.112) | data formatting | bytes 4194304
  180.6 57.0 %all_to_all.64 = f32[32,1,16384]{2,1,0:T(1,128)} all-to-all(f32[32,1,16384]{2,1,0:T(1,128)} %reshape.251), channel_id=1, replica_groups=mesh['row'=8,'col'=32] {'col'}, dimensions={0} | all-to-all | bytes 4194304 | tf_op jit(solution)/shard_map/all_to_all | solution.py:88
  237.6 8.7 %reduce.3 = f32[32,16384]{1,0:T(8,128)} reduce(f32[32,1,16384]{2,1,0:T(1,128)} %all_to_all.64, f32[]{:T(128)} %broadcast.343), dimensions={1}, to_apply=%all_to_all.51.reduce_sub_computation | reduce | bytes 4194308 | tf_op jit(solution)/shard_map/all_to_all | solution.py:88
  246.3 4.2 %reshape.252 = f32[256,2,16,64]{3,2,1,0:T(8,128)} reshape(f32[32,16384]{1,0:T(8,128)} %reduce.3) | data formatting | bytes 4194304
  250.6 7.9 %copy.48 = f32[64,32,16,2,8]{0,4,3,2,1:T(8,128)} copy(f32[64,32,16,2,8]{0,2,3,4,1:T(8,128)} %bitcast.116) | data formatting | bytes 4194304 | tf_op jit(solution)/shard_map/all_to_all | solution.py:88
  258.5 4.7 %copy.60 = f32[64,512,2,8,1]{1,3,2,4,0:T(8,128)} copy(f32[64,512,2,8,1]{0,3,2,1,4:T(8,128)} %bitcast.117) | data formatting | bytes 4194304 | tf_op jit(solution)/shard_map/all_to_all | solution.py:88
  263.2 5.2 %fusion.19 = f32[64,8,2,256]{3,1,2,0:T(8,128)S(1)} fusion(f32[64,512,2,8,1]{1,3,2,4,0:T(8,128)} %copy.60, f32[1,512,2,256]{3,1,0,2:T(8,128)S(1)} %get-tuple-element.8, f32[1,512,2,256]{3,1,0,2:T(8,128)S(1)} %get-tuple-element.7), kind=kOutput, calls=%fused_computation.18 | convolution fusion | flops 3222274048 | bytes 5242880 | tf_op jit(solution)/shard_map/kbpx,pbqy->kxqy/dot_general | solution.py:62
  268.4 1.6 copy.50
  269.9 2.1 reshape.253
  272.1 3.6 %all-to-all-start.4 = ((f32[8,1,32768]{2,1,0:T(1,128)}), f32[8,1,32768]{2,1,0:T(1,128)S(1)}, u32[]{:S(2)}, u32[]{:S(2)}) async-start(f32[8,1,32768]{2,1,0:T(1,128)} %reshape.253), calls=%async_computation.4 | async-start | bytes 2097152 | tf_op jit(solution)/shard_map/all_to_all | solution.py:92
  275.6 2.9 sine_negate_fusion
  278.5 12.9 %all-to-all-done.4 = f32[8,1,32768]{2,1,0:T(1,128)S(1)} async-done(((f32[8,1,32768]{2,1,0:T(1,128)}), f32[8,1,32768]{2,1,0:T(1,128)S(1)}, u32[]{:S(2)}, u32[]{:S(2)}) %all-to-all-start.4) | async-done | bytes 1048608 | tf_op jit(solution)/shard_map/all_to_all | solution.py:92
  291.4 3.1 %reduce.4 = f32[8,32768]{1,0:T(8,128)S(1)} reduce(f32[8,1,32768]{2,1,0:T(1,128)S(1)} %all-to-all-done.4, f32[]{:T(128)} %broadcast.343), dimensions={1}, to_apply=%all_to_all.55.reduce_sub_computation | reduce | bytes 2097156 | tf_op jit(solution)/shard_map/all_to_all | solution.py:92
  294.6 0.8 reshape.254
  295.4 0.0 copy-start.1
  295.4 2.6 copy.52
  298.0 2.0 all_to_all.58
  300.0 1.7 convolution_bitcast_fusion.1
  (11 shorter events, 0.0 us)
Async XLA Ops:
  0.0 3.1 %copy-start = (f32[8,32,256]{2,1,0:T(8,128)S(1)}, f32[8,32,256]{2,1,0:T(8,128)}, u32[]{:S(2)}) copy-start(f32[8,32,256]{2,1,0:T(8,128)} %param.2) | copy-start | bytes 786436
  2.1 0.8 copy-start.3
  2.1 1.0 copy-start.5
  6.7 22.5 %copy-start.4 = (f32[256,1,512]{2,0,1:T(8,128)S(1)}, f32[256,1,512]{2,0,1:T(8,128)}, u32[]{:S(2)}) copy-start(f32[256,1,512]{2,0,1:T(8,128)} %copy-done.3) | copy-start | bytes 1572868
  6.7 22.5 %copy-start.6 = (f32[256,1,512]{2,0,1:T(8,128)S(1)}, f32[256,1,512]{2,0,1:T(8,128)}, u32[]{:S(2)}) copy-start(f32[256,1,512]{2,0,1:T(8,128)} %copy-done.5) | copy-start | bytes 1572868
  6.7 16.2 %all-to-all-start.1 = ((f32[8,1,16384]{2,1,0:T(1,128)}), f32[8,1,16384]{2,1,0:T(1,128)S(1)}, u32[]{:S(2)}, u32[]{:S(2)}) async-start(f32[8,1,16384]{2,1,0:T(1,128)} %reshape.245), calls=%async_computation.1 | async-start | bytes 1048576 | tf_op jit(solution)/shard_map/all_to_all | solution.py:35
  23.0 4.3 %copy-start.8 = (f32[8,1,16384]{2,1,0:T(1,128)}, f32[8,1,16384]{2,1,0:T(1,128)S(1)}, u32[]{:S(2)}) copy-start(f32[8,1,16384]{2,1,0:T(1,128)S(1)} %all-to-all-done.1) | copy-start | bytes 1572868
  23.0 14.7 %all-to-all-start = ((f32[8,1,16384]{2,1,0:T(1,128)}), f32[8,1,16384]{2,1,0:T(1,128)}, u32[]{:S(2)}, u32[]{:S(2)}) async-start(f32[8,1,16384]{2,1,0:T(1,128)} %reshape.247), calls=%async_computation | async-start | bytes 1048576 | tf_op jit(solution)/shard_map/all_to_all | solution.py:35
  29.5 16.0 %copy-start.2 = (f32[1,256,2,512]{3,1,2,0:T(8,128)}, f32[1,256,2,512]{3,1,2,0:T(8,128)S(1)}, u32[]{:S(2)}) copy-start(f32[1,256,2,512]{3,1,2,0:T(8,128)S(1)} %get-tuple-element.10) | copy-start | bytes 3145732
  64.0 61.9 %all-to-all-start.2 = ((f32[32,1,16384]{2,1,0:T(1,128)}), f32[32,1,16384]{2,1,0:T(1,128)}, u32[]{:S(2)}, u32[]{:S(2)}) async-start(f32[32,1,16384]{2,1,0:T(1,128)} %reshape.249), calls=%async_computation.2 | async-start | bytes 4194304 | tf_op jit(solution)/shard_map/all_to_all | solution.py:80
  151.7 9.3 %copy-start.7 = (f32[64,16,512]{2,1,0:T(8,128)S(1)}, f32[64,16,512]{2,1,0:T(8,128)}, u32[]{:S(2)}) copy-start(f32[64,16,512]{2,1,0:T(8,128)} %param.3) | copy-start | bytes 6291460
  272.1 19.4 %all-to-all-start.4 = ((f32[8,1,32768]{2,1,0:T(1,128)}), f32[8,1,32768]{2,1,0:T(1,128)S(1)}, u32[]{:S(2)}, u32[]{:S(2)}) async-start(f32[8,1,32768]{2,1,0:T(1,128)} %reshape.253), calls=%async_computation.4 | async-start | bytes 2097152 | tf_op jit(solution)/shard_map/all_to_all | solution.py:92
  295.4 6.3 %copy-start.1 = (f32[8,32,256]{2,1,0:T(8,128)S(1)}, f32[8,32,256]{2,1,0:T(8,128)}, u32[]{:S(2)}) copy-start(f32[8,32,256]{2,1,0:T(8,128)} %param.2) | copy-start | bytes 786436
  298.0 2.0 copy-start.9
  298.0 2.0 copy-start.10
where the time goes:
time: 308 us; the launch traced here: 302 us
  local copies, waits for them, and re-layouts  77 us (25%)
  waiting for transfers between devices  70 us (23%)
  blocking collectives  57 us (19%)
  other arithmetic  40.9 us (13%)
  matrix products  31 us (10%)
  starting transfers between devices  25.6 us (8%)
    all_to_all x1, blocking collectives, on_device(): lax.all_to_all(back_x, 'col', split_axis=3, concat_axis=1, tiled=True)  57 us
    all_to_all x1, waiting for transfers between devices, on_device(): lax.all_to_all(along_y, 'col', split_axis=3, concat_axis=0, tiled=True)  45.9 us
    unnamed x32, local copies, waits for them, and re-layouts  32.6 us
    dot_general x6, matrix products, contract(): jnp.einsum(pattern, left_side, right_side, precision=lax.Precision.HIGHES...  31 us
    dot_general x3, local copies, waits for them, and re-layouts, contract(): jnp.einsum(pattern, left_side, right_side, precision=lax.Precision.HIGHES...  13.8 us
    all_to_all x1, waiting for transfers between devices, on_device(): lax.all_to_all(back_y, 'row', split_axis=3, concat_axis=0, tiled=True)  12.9 us
    all_to_all x2, local copies, waits for them, and re-layouts, on_device(): lax.all_to_all(back_x, 'col', split_axis=3, concat_axis=1, tiled=True)  12.6 us
    all_to_all x1, starting transfers between devices, on_device(): lax.all_to_all(along_y, 'col', split_axis=3, concat_axis=0, tiled=True)  11.8 us
  transfers between devices with their start and end apart: 4, of which 4 were waited for; matrix products, arithmetic and copies ran while one was open for 5% of the time, Pallas kernels for 0%

commit v1 on v0

v1 whole, which is shorter than its diff:
```python
import functools

import jax
import jax.numpy as jnp
import ml_dtypes
import numpy as np
from jax import lax
from jax.experimental import pallas as pl
from jax.experimental.pallas import tpu as pltpu
from jax.sharding import PartitionSpec as P

M = 512
N = 256
LANES = 128
HALF = 64
BF16 = jnp.bfloat16


def split_table(table):
    high = table.astype(ml_dtypes.bfloat16)
    low = (table - high.astype(np.float64)).astype(ml_dtypes.bfloat16)
    return high, low


@functools.cache
def tables():
    freq = np.arange(M)[:, None]
    cell = np.arange(N)[None, :]
    angle = 2.0 * np.pi * ((freq * cell) % M) / M
    cosine, sine = np.cos(angle), np.sin(angle)
    forward = np.concatenate([cosine, sine], 1)
    backward = np.concatenate([cosine.T, sine.T], 0)
    return split_table(forward) + split_table(backward)


def halves(value):
    high = value.astype(BF16)
    low = (value - high.astype(jnp.float32)).astype(BF16)
    return high, low


def mul(left, right, dims=((1,), (0,))):
    dot = functools.partial(
        lax.dot_general, dimension_numbers=(dims, ((), ())), preferred_element_type=jnp.float32
    )
    (lh, ll), (rh, rl) = left, right
    return dot(lh, rh) + (dot(lh, rl) + dot(ll, rh))


def swap_parts(value):
    return pltpu.roll(value, HALF, 1)


def real_lanes(shape):
    return lax.broadcasted_iota(jnp.int32, shape, 1) < HALF


def forward_rows(data):
    turned = swap_parts(data)
    turned = jnp.where(real_lanes(data.shape), turned, -turned)
    return jnp.concatenate([data, turned], 0)


def backward_join(both):
    n = both.shape[0] // 2
    even, odd = both[:n], swap_parts(both[n:])
    return even + jnp.where(real_lanes(odd.shape), -odd, odd)


def z_rows(table, r):
    rows = slice(HALF * r, HALF * (r + 1))
    return jnp.concatenate([table[rows, :N], -table[rows, N:]], 0)


def z_forward(charge, th, tl, out):
    value = halves(charge[...])
    for r in range(out.shape[0]):
        out[r] = mul(value, (z_rows(th, r), z_rows(tl, r)), ((1,), (1,)))


def y_forward(data, th, tl, out):
    table = (th[...], tl[...])

    def step(k, carry):
        cols = [
            forward_rows(data[:, 2 * k + i].reshape(N, LANES)) for i in range(2)
        ]
        both = mul(table, halves(jnp.concatenate(cols, 1)))
        for i in range(2):
            out[:, 2 * k + i] = both[:, LANES * i : LANES * (i + 1)].reshape(32, 16, LANES)
        return carry

    lax.fori_loop(0, 4, step, 0)


def x_both(data, green, fh, fl, bh, bl, out):
    forward = (fh[...], fl[...])
    backward = (bh[...], bl[...])

    def step(k, carry):
        cols = [
            forward_rows(data[pl.ds(2 * k + i, N, stride=16), :]) for i in range(2)
        ]
        spectrum = mul(forward, halves(jnp.concatenate(cols, 1)))
        product = spectrum * jnp.concatenate([green[2 * k + i] for i in range(2)], 1)
        both = mul(backward, halves(product))
        for i in range(2):
            field = backward_join(both[:, LANES * i : LANES * (i + 1)])
            out[:, 2 * k + i] = field.reshape(32, 8, LANES)
        return carry

    lax.fori_loop(0, 8, step, 0)


def y_backward(data, bh, bl, out):
    backward = (bh[...], bl[...])

    def step(k, carry):
        cols = [data[pl.ds(2 * k + i, M, stride=8), :] for i in range(2)]
        both = mul(backward, halves(jnp.concatenate(cols, 1)))
        for i in range(2):
            field = backward_join(both[:, LANES * i : LANES * (i + 1)])
            out[:, 2 * k + i] = field.reshape(8, 32, LANES)
        return carry

    lax.fori_loop(0, 4, step, 0)


def z_backward(data, th, tl, out):
    total = 0.0
    for r in range(data.shape[0]):
        total += mul(halves(data[r]), (z_rows(th, r), z_rows(tl, r)))
    out[...] = total * (1.0 / M**3)


def turn_green(green, out):
    for b in range(16):
        part = green[:, b, :]
        out[b] = jnp.concatenate([part, part], 0).T


def call(body, shape, flops, *args):
    return pl.pallas_call(
        body,
        out_shape=jax.ShapeDtypeStruct(shape, jnp.float32),
        in_specs=[pl.BlockSpec(memory_space=pltpu.VMEM)] * len(args),
        out_specs=pl.BlockSpec(memory_space=pltpu.VMEM),
        compiler_params=pltpu.CompilerParams(vmem_limit_bytes=48 * 1024 * 1024),
        cost_estimate=pl.CostEstimate(
            flops=flops, bytes_accessed=4 * int(np.prod(shape)), transcendentals=0
        ),
        name=body.__name__,
    )(*args)


def exchange(value, axis):
    return lax.all_to_all(value, axis, split_axis=0, concat_axis=0, tiled=True)


def on_device(charge, green_spectrum):
    fh, fl, bh, bl = (jnp.asarray(t) for t in tables())
    green = call(turn_green, (16, M, LANES), 10**9, green_spectrum)
    along_z = call(z_forward, (8, 256, LANES), 10**9, charge.reshape(256, N), fh, fl)
    by_rows = exchange(along_z, "row")
    along_y = call(
        y_forward, (32, 8, 16, LANES), 10**9, by_rows.reshape(8, 8, 32, LANES), fh, fl
    )
    by_cols = exchange(along_y.reshape(32, LANES, LANES), "col")
    back_x = call(
        x_both, (32, 16, 8, LANES), 10**9, by_cols.reshape(4096, LANES), green, fh, fl, bh, bl
    )
    by_cells = exchange(back_x.reshape(32, LANES, LANES), "col")
    back_y = call(
        y_backward, (8, 8, 32, LANES), 10**9, by_cells.reshape(4096, LANES), bh, bl
    )
    by_parts = exchange(back_y.reshape(8, 256, LANES), "row")
    back_z = call(z_backward, (256, N), 10**9, by_parts, fh, fl)
    return back_z.reshape(8, 32, N)


def solution(mesh):
    in_specs = (P("col", "row", None), P("row", "col", None))
    out_specs = P("col", "row", None)
    return jax.shard_map(
        on_device, mesh=mesh, in_specs=in_specs, out_specs=out_specs, check_vma=False
    )
```

time: 308 us -> 192 us (0.62); the launches traced: 302 us -> 191 us
  local copies, waits for them, and re-layouts: 77 us -> 5.14 us
  other arithmetic: 40.9 us -> 0 us
  blocking collectives: 57 us -> 94.6 us
  Pallas kernels: 0 us -> 31.4 us
  matrix products: 31 us -> 0 us
  waiting for transfers between devices: 70 us -> 46.9 us
  starting transfers between devices: 25.6 us -> 13 us
    all_to_all x1 -> x3, blocking collectives: 57 us -> 94.6 us  [exchange(): return lax.all_to_all(value, axis, split_axis=0, concat_axis=0, tiled=True)]
    pallas_call x0 -> x6, Pallas kernels: none -> 31.4 us  [call(): pl.pallas_call(body, out_shape=jax.ShapeDtypeStruct(shape, jnp.float32),...]
    dot_general x6 -> x0, matrix products: 31 us -> none  [contract(): jnp.einsum(pattern, left_side, right_side, precision=lax.Precision.HIGHES...]
    all_to_all x8 -> x0, local copies, waits for them, and re-layouts: 29.2 us -> none  [the longest x2 12.6 us: on_device(): lax.all_to_all(back_x, 'col', split_axis=3, concat_axis=1, tiled=True)]
    all_to_all x5 -> x0, other arithmetic: 28.1 us -> none  [the longest x1 8.73 us: on_device(): lax.all_to_all(back_x, 'col', split_axis=3, concat_axis=1, tiled=True)]
    unnamed x32 -> x18, local copies, waits for them, and re-layouts: 32.6 us -> 5.14 us
    all_to_all x4 -> x1, waiting for transfers between devices: 70 us -> 46.9 us  [exchange(): return lax.all_to_all(value, axis, split_axis=0, concat_axis=0, tiled=True)]
    dot_general x3 -> x0, local copies, waits for them, and re-layouts: 13.8 us -> none  [contract(): jnp.einsum(pattern, left_side, right_side, precision=lax.Precision.HIGHES...]
  transfers between devices with their start and end apart: 4 -> 1, of which waited for: 4 -> 1; matrix products, arithmetic and copies ran while one was open for 5% -> 0% of each run, Pallas kernels for 0% -> 2%
where the time goes in v1:
time: 192 us; the launch traced here: 191 us
  blocking collectives  94.6 us (49%)
  waiting for transfers between devices  46.9 us (24%)
  Pallas kernels  31.4 us (16%)
  starting transfers between devices  13 us (7%)
  local copies, waits for them, and re-layouts  5.14 us (3%)
    all_to_all x3, blocking collectives, exchange(): return lax.all_to_all(value, axis, split_axis=0, concat_axis=0, tiled=True)  94.6 us
    all_to_all x1, waiting for transfers between devices, exchange(): return lax.all_to_all(value, axis, split_axis=0, concat_axis=0, tiled=True)  46.9 us
    pallas_call x6, Pallas kernels, call(): pl.pallas_call(body, out_shape=jax.ShapeDtypeStruct(shape, jnp.float32),...  31.4 us
    all_to_all x1, starting transfers between devices, exchange(): return lax.all_to_all(value, axis, split_axis=0, concat_axis=0, tiled=True)  13 us
    unnamed x18, local copies, waits for them, and re-layouts  5.14 us
  transfers between devices with their start and end apart: 1, of which 1 were waited for; matrix products, arithmetic and copies ran while one was open for 0% of the time, Pallas kernels for 2%

profile of v1, /device:TPU:1, one launch (start us, length us, event | category | flops | bytes accessed | tf_op | source)
XLA Modules:
  0.0 191.1 jit_solution(3728541719149739908)
XLA Ops:
  0.0 0.0 copy-start.1
  0.0 1.0 copy-done.1
  1.0 0.0 copy-start.3
  1.0 1.0 copy-done.3
  2.1 0.0 copy-start.8
  2.1 0.9 copy-done.8
  3.0 0.0 copy-start.2
  3.0 1.0 z_forward.1
  4.0 20.5 %all_to_all.20 = f32[8,256,128]{2,1,0:T(8,128)S(1)} all-to-all(f32[8,256,128]{2,1,0:T(8,128)S(1)} %z_forward.1), channel_id=1, replica_groups=mesh['row'=8,'col'=32] {'row'}, dimensions={0} | all-to-all | bytes 2097152 | tf_op jit(solution)/shard_map/all_to_all | solution.py:157
  24.5 0.0 copy-done.2
  24.5 4.1 %y_forward.1 = f32[32,8,16,128]{3,2,1,0:T(8,128)} custom-call(f32[8,8,32,128]{3,2,1,0:T(8,128)S(1)} %bitcast.11, bf16[512,512]{1,0:T(8,128)(2,1)S(1)} %copy-done.3, bf16[512,512]{1,0:T(8,128)(2,1)S(1)} %copy-done.2), custom_call_target="tpu_custom_call" | custom-call | flops 1000000000 | bytes 2097152 | tf_op jit(solution)/shard_map/y_forward/pallas_call | solution.py:143
  28.6 0.0 copy-start
  28.6 13.0 %all-to-all-start.1 = ((f32[32,128,128]{2,1,0:T(8,128)}), f32[32,128,128]{2,1,0:T(8,128)}, u32[]{:S(2)}, u32[]{:S(2)}) async-start(f32[32,128,128]{2,1,0:T(8,128)} %bitcast.2), calls=%async_computation.1 | async-start | bytes 4194304 | tf_op jit(solution)/shard_map/all_to_all | solution.py:157
  41.6 0.0 copy-done
  41.6 0.0 copy-start.4
  41.6 3.1 %turn_green.1.green = f32[16,512,128]{2,1,0:T(8,128)} custom-call(f32[64,16,512]{2,1,0:T(8,128)S(1)} %copy-done), custom_call_target="tpu_custom_call" | custom-call | flops 1000000000 | bytes 4194304 | tf_op jit(solution)/shard_map/turn_green/pallas_call | solution.py:143
  44.7 46.9 %all-to-all-done.1 = f32[32,128,128]{2,1,0:T(8,128)} async-done(((f32[32,128,128]{2,1,0:T(8,128)}), f32[32,128,128]{2,1,0:T(8,128)}, u32[]{:S(2)}, u32[]{:S(2)}) %all-to-all-start.1) | async-done | bytes 2097184 | tf_op jit(solution)/shard_map/all_to_all | solution.py:157
  91.7 0.0 copy-done.4
  91.7 0.0 copy-start.5
  91.7 1.0 copy-done.5
  92.7 0.0 copy-start.7
  92.7 1.0 copy-done.7
  93.8 18.6 %x_both.1 = f32[32,16,8,128]{3,2,1,0:T(8,128)S(1)} custom-call(f32[4096,128]{1,0:T(8,128)} %bitcast.3.data, f32[16,512,128]{2,1,0:T(8,128)} %turn_green.1.green, bf16[512,512]{1,0:T(8,128)(2,1)S(1)} %copy-done.4, bf16[512,512]{1,0:T(8,128)(2,1)S(1)} %copy-done.2, bf16[512,512]{1,0:T(8,128)(2,1)S(1)} %copy-done.7, bf16[512,512]{1,0:T(8,128)(2,1)S(1)} %copy-done.5), custom_call_target="tpu_custom_call" | custom-call | flops 1000000000 | bytes 2097152 | tf_op jit(solution)/shard_map/x_both/pallas_call | solution.py:143
  112.4 0.0 copy-start.6
  112.4 56.8 %all_to_all.21 = f32[32,128,128]{2,1,0:T(8,128)S(1)} all-to-all(f32[32,128,128]{2,1,0:T(8,128)S(1)} %bitcast.8), channel_id=1, replica_groups=mesh['row'=8,'col'=32] {'col'}, dimensions={0} | all-to-all | bytes 4194304 | tf_op jit(solution)/shard_map/all_to_all | solution.py:157
  169.2 0.0 copy-done.6
  169.2 2.9 %y_backward.1 = f32[8,8,32,128]{3,2,1,0:T(8,128)S(1)} custom-call(f32[4096,128]{1,0:T(8,128)S(1)} %bitcast.9, bf16[512,512]{1,0:T(8,128)(2,1)S(1)} %copy-done.7, bf16[512,512]{1,0:T(8,128)(2,1)S(1)} %copy-done.6), custom_call_target="tpu_custom_call" | custom-call | flops 1000000000 | bytes 1048576 | tf_op jit(solution)/shard_map/y_backward/pallas_call | solution.py:143
  172.2 17.3 %all_to_all.22.data = f32[8,256,128]{2,1,0:T(8,128)S(1)} all-to-all(f32[8,256,128]{2,1,0:T(8,128)S(1)} %bitcast.10), channel_id=1, replica_groups=mesh['row'=8,'col'=32] {'row'}, dimensions={0} | all-to-all | bytes 2097152 | tf_op jit(solution)/shard_map/all_to_all | solution.py:157
  189.4 1.7 z_backward.1
Async XLA Ops:
  0.0 1.0 copy-start.1
  1.0 1.0 copy-start.3
  2.1 0.9 copy-start.8
  3.0 21.5 %copy-start.2 = (bf16[512,512]{1,0:T(8,128)(2,1)S(1)}, bf16[512,512]{1,0:T(8,128)(2,1)}, u32[]{:S(2)}) copy-start(bf16[512,512]{1,0:T(8,128)(2,1)} %constant.9.clone.tl.fl) | copy-start | bytes 1572868
  28.6 13.0 %copy-start = (f32[64,16,512]{2,1,0:T(8,128)S(1)}, f32[64,16,512]{2,1,0:T(8,128)}, u32[]{:S(2)}) copy-start(f32[64,16,512]{2,1,0:T(8,128)} %green.1) | copy-start | bytes 6291460
  28.6 63.1 %all-to-all-start.1 = ((f32[32,128,128]{2,1,0:T(8,128)}), f32[32,128,128]{2,1,0:T(8,128)}, u32[]{:S(2)}, u32[]{:S(2)}) async-start(f32[32,128,128]{2,1,0:T(8,128)} %bitcast.2), calls=%async_computation.1 | async-start | bytes 4194304 | tf_op jit(solution)/shard_map/all_to_all | solution.py:157
  41.6 50.1 %copy-start.4 = (bf16[512,512]{1,0:T(8,128)(2,1)S(1)}, bf16[512,512]{1,0:T(8,128)(2,1)}, u32[]{:S(2)}) copy-start(bf16[512,512]{1,0:T(8,128)(2,1)} %constant.8.clone.th.fh) | copy-start | bytes 1572868
  91.7 1.0 copy-start.5
  92.7 1.0 copy-start.7
  112.4 56.9 %copy-start.6 = (bf16[512,512]{1,0:T(8,128)(2,1)S(1)}, bf16[512,512]{1,0:T(8,128)(2,1)}, u32[]{:S(2)}) copy-start(bf16[512,512]{1,0:T(8,128)(2,1)} %constant.11.clone.bl) | copy-start | bytes 1572868

commit v2 on v1

v2 whole, which is shorter than its diff:
```python
import functools

import jax
import jax.numpy as jnp
import ml_dtypes
import numpy as np
from jax import lax
from jax.experimental import pallas as pl
from jax.experimental.pallas import tpu as pltpu
from jax.sharding import PartitionSpec as P

M = 512
N = 256
LANES = 128
HALF = 64
BF16 = jnp.bfloat16


def split_table(table):
    high = table.astype(ml_dtypes.bfloat16)
    low = (table - high.astype(np.float64)).astype(ml_dtypes.bfloat16)
    return high, low


@functools.cache
def tables():
    freq = np.arange(N)[:, None]
    pair = np.arange(N // 2)[None, :]
    forward = []
    for parity in range(2):
        angle = 2.0 * np.pi * ((freq * (2 * pair + parity)) % M) / M
        forward.append(np.concatenate([np.cos(angle), np.sin(angle)], 1))
    forward = np.stack(forward)
    angle = 2.0 * np.pi * ((np.arange(M)[:, None] * np.arange(N)[None, :]) % M) / M
    angle = angle.reshape(8, HALF, N)
    along_z = np.concatenate([np.cos(angle), -np.sin(angle)], 1).reshape(2 * M, N)
    return tuple(
        np.stack(split_table(t)) for t in (along_z, forward, forward.transpose(0, 2, 1))
    )


def halves(value):
    high = value.astype(BF16)
    low = (value - high.astype(jnp.float32)).astype(BF16)
    return high, low


def mul(left, right, dims=((1,), (0,))):
    dot = functools.partial(
        lax.dot_general, dimension_numbers=(dims, ((), ())), preferred_element_type=jnp.float32
    )
    (lh, ll), (rh, rl) = left, right
    return dot(lh, rh) + (dot(lh, rl) + dot(ll, rh))


def swap_parts(value):
    return pltpu.roll(value, HALF, 1)


def real_lanes(shape):
    return lax.broadcasted_iota(jnp.int32, shape, 1) < HALF


def forward_rows(data):
    turned = swap_parts(data)
    turned = jnp.where(real_lanes(data.shape), turned, -turned)
    return jnp.concatenate([data, turned], 0)


def backward_join(both):
    n = both.shape[0] // 2
    even, odd = both[:n], swap_parts(both[n:])
    return even + jnp.where(real_lanes(odd.shape), -odd, odd)


def z_forward(charge, table, out):
    value = halves(charge[...])
    for r in range(out.shape[0]):
        rows = slice(LANES * r, LANES * (r + 1))
        out[r] = mul(value, (table[0, rows], table[1, rows]), ((1,), (1,)))


def both_parities(table, cols):
    return [
        mul((table[0, p], table[1, p]), halves(jnp.concatenate([forward_rows(c) for c in cols[p]], 1)))
        for p in range(2)
    ]


def y_forward(data, table, out):
    def step(k, carry):
        cols = [
            [
                jnp.concatenate(
                    [data[pl.ds(256 * s + 32 * (2 * k + i) + p, 16, stride=2), :] for s in range(8)], 0
                )
                for i in range(2)
            ]
            for p in range(2)
        ]
        even, odd = both_parities(table, cols)
        for i in range(2):
            at = slice(LANES * i, LANES * (i + 1))
            low, high = even[:, at] + odd[:, at], even[:, at] - odd[:, at]
            out[:16, 2 * k + i] = low.reshape(16, 16, LANES)
            out[16:, 2 * k + i] = high.reshape(16, 16, LANES)
        return carry

    lax.fori_loop(0, 4, step, 0, unroll=2)


def x_both(data, green, forward, backward, out):
    def step(k, carry):
        cols = [
            [data[pl.ds(16 * p + 2 * k + i, LANES, stride=32), :] for i in range(2)]
            for p in range(2)
        ]
        even, odd = both_parities(forward, cols)
        low, high = (
            jnp.concatenate([green[2 * k + i, N * h : N * (h + 1)] for i in range(2)], 1)
            for h in range(2)
        )
        low, high = (even + odd) * low, (even - odd) * high
        for p, value in enumerate((low + high, low - high)):
            both = mul((backward[0, p], backward[1, p]), halves(value))
            for i in range(2):
                field = backward_join(both[:, LANES * i : LANES * (i + 1)])
                out[pl.ds(16 * p + 2 * k + i, LANES, stride=32), :] = field
        return carry

    lax.fori_loop(0, 8, step, 0, unroll=2)


def y_backward(data, backward, out):
    def step(k, carry):
        low, high = (
            jnp.concatenate(
                [data[16 * h : 16 * (h + 1), 2 * k + i].reshape(N, LANES) for i in range(2)], 1
            )
            for h in range(2)
        )
        for p, value in enumerate((low + high, low - high)):
            both = mul((backward[0, p], backward[1, p]), halves(value))
            for i in range(2):
                field = backward_join(both[:, LANES * i : LANES * (i + 1)])
                for s in range(8):
                    rows = pl.ds(256 * s + 32 * (2 * k + i) + p, 16, stride=2)
                    out[rows, :] = field[16 * s : 16 * (s + 1)]
        return carry

    lax.fori_loop(0, 4, step, 0, unroll=2)


def z_backward(data, table, out):
    total = 0.0
    for r in range(data.shape[0]):
        rows = slice(LANES * r, LANES * (r + 1))
        total += mul(halves(data[r]), (table[0, rows], table[1, rows]))
    out[...] = total * (1.0 / M**3)


def turn_green(green, out):
    for b in range(16):
        part = green[:, b, :]
        out[b] = jnp.concatenate([part, part], 0).T


def call(body, shape, grant, *args):
    return pl.pallas_call(
        body,
        out_shape=jax.ShapeDtypeStruct(shape, jnp.float32),
        in_specs=[pl.BlockSpec(memory_space=pltpu.VMEM)] * len(args),
        out_specs=pl.BlockSpec(memory_space=pltpu.VMEM),
        compiler_params=pltpu.CompilerParams(vmem_limit_bytes=grant * 1024 * 1024),
        cost_estimate=pl.CostEstimate(
            flops=10**9, bytes_accessed=4 * int(np.prod(shape)), transcendentals=0
        ),
        name=body.__name__,
    )(*args)


def exchange(value, axis):
    return lax.all_to_all(value, axis, split_axis=0, concat_axis=0, tiled=True)


def on_device(charge, green_spectrum):
    z_table, forward, backward = (jnp.asarray(t) for t in tables())
    green = call(turn_green, (16, M, LANES), 60, green_spectrum)
    along_z = call(z_forward, (8, 256, LANES), 60, charge.reshape(256, N), z_table)
    by_rows = exchange(along_z, "row").reshape(2048, LANES)
    along_y = call(y_forward, (32, 8, 16, LANES), 60, by_rows, forward)
    by_cols = exchange(along_y.reshape(32, LANES, LANES), "col").reshape(4096, LANES)
    back_x = call(x_both, (4096, LANES), 16, by_cols, green, forward, backward)
    by_cells = exchange(back_x.reshape(32, LANES, LANES), "col")
    back_y = call(
        y_backward, (2048, LANES), 16, by_cells.reshape(32, 8, 16, LANES), backward
    )
    by_parts = exchange(back_y.reshape(8, 256, LANES), "row")
    back_z = call(z_backward, (256, N), 16, by_parts, z_table)
    return back_z.reshape(8, 32, N)


def solution(mesh):
    in_specs = (P("col", "row", None), P("row", "col", None))
    out_specs = P("col", "row", None)
    return jax.shard_map(
        on_device, mesh=mesh, in_specs=in_specs, out_specs=out_specs, check_vma=False
    )
```

time: 192 us -> 179 us (0.932)
  Pallas kernels: 31.4 us -> 23.1 us
  local copies, waits for them, and re-layouts: 5.14 us -> 2.21 us
    pallas_call x6, Pallas kernels: 31.4 us -> 23.1 us  [call(): pl.pallas_call(body, out_shape=jax.ShapeDtypeStruct(shape, jnp.float32),...]
    unnamed x18 -> x8, local copies, waits for them, and re-layouts: 5.14 us -> 2.21 us
  transfers between devices with their start and end apart: 1 -> 1, of which waited for: 1 -> 1; matrix products, arithmetic and copies ran while one was open for 0% -> 0% of each run, Pallas kernels for 2% -> 3%
where the time goes in v2:
time: 179 us; the launch traced here: 178 us
  blocking collectives  94.5 us (53%)
  waiting for transfers between devices  45.2 us (25%)
  Pallas kernels  23.1 us (13%)
  starting transfers between devices  13.1 us (7%)
  local copies, waits for them, and re-layouts  2.21 us (1%)
    all_to_all x3, blocking collectives, exchange(): return lax.all_to_all(value, axis, split_axis=0, concat_axis=0, tiled=True)  94.5 us
    all_to_all x1, waiting for transfers between devices, exchange(): return lax.all_to_all(value, axis, split_axis=0, concat_axis=0, tiled=True)  45.2 us
    pallas_call x6, Pallas kernels, call(): pl.pallas_call(body, out_shape=jax.ShapeDtypeStruct(shape, jnp.float32),...  23.1 us
    all_to_all x1, starting transfers between devices, exchange(): return lax.all_to_all(value, axis, split_axis=0, concat_axis=0, tiled=True)  13.1 us
  transfers between devices with their start and end apart: 1, of which 1 were waited for; matrix products, arithmetic and copies ran while one was open for 0% of the time, Pallas kernels for 3%

profile of v2, /device:TPU:1, one launch (start us, length us, event | category | flops | bytes accessed | tf_op | source)
XLA Modules:
  0.0 178.1 jit_solution(8235681206801932187)
XLA Ops:
  0.0 3.3 %z_forward.1 = f32[8,256,128]{2,1,0:T(8,128)} custom-call(f32[256,256]{1,0:T(8,128)} %bitcast.14, bf16[2,1024,256]{2,1,0:T(8,128)(2,1)} %constant.6.clone.table), custom_call_target="tpu_custom_call" | custom-call | flops 1000000000 | bytes 1048576 | tf_op jit(solution)/shard_map/z_forward/pallas_call | solution.py:169
  3.3 20.5 %all_to_all.20 = f32[8,256,128]{2,1,0:T(8,128)} all-to-all(f32[8,256,128]{2,1,0:T(8,128)} %z_forward.1), channel_id=1, replica_groups=mesh['row'=8,'col'=32] {'row'}, dimensions={0} | all-to-all | bytes 2097152 | tf_op jit(solution)/shard_map/all_to_all | solution.py:183
  23.8 4.1 %y_forward.1 = f32[32,8,16,128]{3,2,1,0:T(8,128)} custom-call(f32[2048,128]{1,0:T(8,128)} %bitcast.13, bf16[2,2,256,256]{3,2,1,0:T(8,128)(2,1)} %constant.7.clone.table.forward), custom_call_target="tpu_custom_call" | custom-call | flops 1000000000 | bytes 2097152 | tf_op jit(solution)/shard_map/y_forward/pallas_call | solution.py:169
  27.9 13.1 %all-to-all-start.1 = ((f32[32,128,128]{2,1,0:T(8,128)}), f32[32,128,128]{2,1,0:T(8,128)S(1)}, u32[]{:S(2)}, u32[]{:S(2)}) async-start(f32[32,128,128]{2,1,0:T(8,128)} %bitcast.12), calls=%async_computation.1 | async-start | bytes 4194304 | tf_op jit(solution)/shard_map/all_to_all | solution.py:183
  41.0 0.0 copy-start.1
  41.0 0.0 copy-start.2
  41.0 4.8 %turn_green.1.green = f32[16,512,128]{2,1,0:T(8,128)} custom-call(f32[64,16,512]{2,1,0:T(8,128)} %green.1), custom_call_target="tpu_custom_call" | custom-call | flops 1000000000 | bytes 4194304 | tf_op jit(solution)/shard_map/turn_green/pallas_call | solution.py:169
  45.8 45.2 %all-to-all-done.1 = f32[32,128,128]{2,1,0:T(8,128)S(1)} async-done(((f32[32,128,128]{2,1,0:T(8,128)}), f32[32,128,128]{2,1,0:T(8,128)S(1)}, u32[]{:S(2)}, u32[]{:S(2)}) %all-to-all-start.1) | async-done | bytes 2097184 | tf_op jit(solution)/shard_map/all_to_all | solution.py:183
  91.0 0.0 copy-done.1
  91.0 0.0 copy-done.2
  91.0 0.0 copy-start
  91.0 2.2 %copy-done = f32[16,512,128]{2,1,0:T(8,128)S(1)} copy-done((f32[16,512,128]{2,1,0:T(8,128)S(1)}, f32[16,512,128]{2,1,0:T(8,128)}, u32[]{:S(2)}) %copy-start) | copy-done | bytes 4194328
  93.2 7.8 %x_both.1 = f32[4096,128]{1,0:T(8,128)S(1)} custom-call(f32[4096,128]{1,0:T(8,128)S(1)} %bitcast.8, f32[16,512,128]{2,1,0:T(8,128)S(1)} %copy-done, bf16[2,2,256,256]{3,2,1,0:T(8,128)(2,1)S(1)} %copy-done.2, bf16[2,2,256,256]{3,2,1,0:T(8,128)(2,1)S(1)} %copy-done.1), custom_call_target="tpu_custom_call" | custom-call | flops 1000000000 | bytes 2097152 | tf_op jit(solution)/shard_map/x_both/pallas_call | solution.py:169
  101.0 56.7 %all_to_all.21 = f32[32,128,128]{2,1,0:T(8,128)S(1)} all-to-all(f32[32,128,128]{2,1,0:T(8,128)S(1)} %bitcast.9), channel_id=1, replica_groups=mesh['row'=8,'col'=32] {'col'}, dimensions={0} | all-to-all | bytes 4194304 | tf_op jit(solution)/shard_map/all_to_all | solution.py:183
  157.7 0.0 copy-start.3
  157.7 1.4 y_backward.1
  159.2 17.3 %all_to_all.22.data = f32[8,256,128]{2,1,0:T(8,128)S(1)} all-to-all(f32[8,256,128]{2,1,0:T(8,128)S(1)} %bitcast.11), channel_id=1, replica_groups=mesh['row'=8,'col'=32] {'row'}, dimensions={0} | all-to-all | bytes 2097152 | tf_op jit(solution)/shard_map/all_to_all | solution.py:183
  176.4 0.0 copy-done.3
  176.4 1.7 z_backward.1
Async XLA Ops:
  27.9 63.1 %all-to-all-start.1 = ((f32[32,128,128]{2,1,0:T(8,128)}), f32[32,128,128]{2,1,0:T(8,128)S(1)}, u32[]{:S(2)}, u32[]{:S(2)}) async-start(f32[32,128,128]{2,1,0:T(8,128)} %bitcast.12), calls=%async_computation.1 | async-start | bytes 4194304 | tf_op jit(solution)/shard_map/all_to_all | solution.py:183
  41.0 50.1 %copy-start.1 = (bf16[2,2,256,256]{3,2,1,0:T(8,128)(2,1)S(1)}, bf16[2,2,256,256]{3,2,1,0:T(8,128)(2,1)}, u32[]{:S(2)}) copy-start(bf16[2,2,256,256]{3,2,1,0:T(8,128)(2,1)} %constant.8.clone.backward) | copy-start | bytes 1572868
  41.0 50.1 %copy-start.2 = (bf16[2,2,256,256]{3,2,1,0:T(8,128)(2,1)S(1)}, bf16[2,2,256,256]{3,2,1,0:T(8,128)(2,1)}, u32[]{:S(2)}) copy-start(bf16[2,2,256,256]{3,2,1,0:T(8,128)(2,1)} %constant.7.clone.table.forward) | copy-start | bytes 1572868
  91.0 2.2 %copy-start = (f32[16,512,128]{2,1,0:T(8,128)S(1)}, f32[16,512,128]{2,1,0:T(8,128)}, u32[]{:S(2)}) copy-start(f32[16,512,128]{2,1,0:T(8,128)} %turn_green.1.green) | copy-start | bytes 12582916
  157.7 18.7 %copy-start.3 = (bf16[2,1024,256]{2,1,0:T(8,128)(2,1)S(1)}, bf16[2,1024,256]{2,1,0:T(8,128)(2,1)}, u32[]{:S(2)}) copy-start(bf16[2,1024,256]{2,1,0:T(8,128)(2,1)} %constant.6.clone.table) | copy-start | bytes 3145732

commit v3 on v2

v3 whole, which is shorter than its diff:
```python
import functools

import jax
import jax.numpy as jnp
import ml_dtypes
import numpy as np
from jax import lax
from jax.experimental import pallas as pl
from jax.experimental.pallas import tpu as pltpu
from jax.sharding import PartitionSpec as P

M = 512
N = 256
LANES = 128
HALF = 64
SLOTS = 32
BF16 = jnp.bfloat16


def split_table(table):
    high = table.astype(ml_dtypes.bfloat16)
    low = (table - high.astype(np.float64)).astype(ml_dtypes.bfloat16)
    return high, low


@functools.cache
def tables():
    freq = np.arange(N)[:, None]
    pair = np.arange(N // 2)[None, :]
    forward = []
    for parity in range(2):
        angle = 2.0 * np.pi * ((freq * (2 * pair + parity)) % M) / M
        forward.append(np.concatenate([np.cos(angle), np.sin(angle)], 1))
    forward = np.stack(forward)
    freq = np.arange(8)[:, None] * HALF + np.arange(SLOTS)[None, :]
    freq[:4, 0] += SLOTS
    angle = 2.0 * np.pi * ((freq[:, :, None] * np.arange(N)) % M) / M
    back_z = np.concatenate([np.cos(angle), -np.sin(angle)], 1).reshape(M, N)
    own = np.concatenate([freq == N, freq == N], 1).reshape(M, 1)
    along_z = np.where(own, 0.5, 1.0) * back_z
    return tuple(
        np.stack(split_table(t)) for t in (along_z, back_z, forward, forward.transpose(0, 2, 1))
    )


def halves(value):
    high = value.astype(BF16)
    low = (value - high.astype(jnp.float32)).astype(BF16)
    return high, low


def mul(left, right, dims=((1,), (0,))):
    dot = functools.partial(
        lax.dot_general, dimension_numbers=(dims, ((), ())), preferred_element_type=jnp.float32
    )
    (lh, ll), (rh, rl) = left, right
    return dot(lh, rh) + (dot(lh, rl) + dot(ll, rh))


def real_lanes(value):
    return lax.broadcasted_iota(jnp.int32, value.shape, 1) % HALF < SLOTS


def forward_rows(data):
    after, before = pltpu.roll(data, LANES - SLOTS, 1), pltpu.roll(data, SLOTS, 1)
    return jnp.concatenate([data, jnp.where(real_lanes(data), after, -before)], 0)


def backward_join(both):
    n = both.shape[0] // 2
    sine = both[n:]
    after, before = pltpu.roll(sine, LANES - SLOTS, 1), pltpu.roll(sine, SLOTS, 1)
    return both[:n] + jnp.where(real_lanes(sine), -after, before)


def trade(first, second):
    low = lax.broadcasted_iota(jnp.int32, first.shape, 1) < HALF
    turned = [pltpu.roll(v, HALF, 1) for v in (first, second)]
    return jnp.where(low, first, turned[1]), jnp.where(low, turned[0], second)


def z_forward(charge, table, out):
    value = halves(charge[...])
    for q in range(4):
        rows = slice(LANES * q, LANES * (q + 1))
        pair = mul(value, (table[0, rows], table[1, rows]), ((1,), (1,)))
        out[2 * q], out[2 * q + 1] = trade(pair[:LANES], pair[LANES:])


def both_parities(table, cols):
    return [
        mul((table[0, p], table[1, p]), halves(jnp.concatenate([forward_rows(c) for c in cols[p]], 1)))
        for p in range(2)
    ]


def y_forward(data, table, out):
    for k in range(2):
        cols = [
            [
                jnp.concatenate(
                    [data[pl.ds(128 * s + 32 * (2 * k + i) + p, 16, stride=2), :] for s in range(8)], 0
                )
                for i in range(2)
            ]
            for p in range(2)
        ]
        even, odd = both_parities(table, cols)
        for i in range(2):
            at = slice(LANES * i, LANES * (i + 1))
            for h, value in enumerate((even[:, at] + odd[:, at], even[:, at] - odd[:, at])):
                value = value.reshape(16, 2, 8, LANES)
                pair = trade(value[:, 0].reshape(LANES, LANES), value[:, 1].reshape(LANES, LANES))
                for x in range(2):
                    out[16 * h : 16 * (h + 1), 4 * x + 2 * k + i] = pair[x].reshape(16, 8, LANES)


def x_both(data, green, forward, backward, out):
    def step(k, carry):
        cols = [
            [data[pl.ds(8 * p + 2 * k + i, LANES, stride=16), :] for i in range(2)]
            for p in range(2)
        ]
        even, odd = both_parities(forward, cols)
        low, high = (
            jnp.concatenate([green[2 * k + i, N * h : N * (h + 1)] for i in range(2)], 1)
            for h in range(2)
        )
        low, high = (even + odd) * low, (even - odd) * high
        for p, value in enumerate((low + high, low - high)):
            both = mul((backward[0, p], backward[1, p]), halves(value))
            for i in range(2):
                field = backward_join(both[:, LANES * i : LANES * (i + 1)])
                out[pl.ds(8 * p + 2 * k + i, LANES, stride=16), :] = field
        return carry

    lax.fori_loop(0, 4, step, 0, unroll=2)


def y_backward(data, backward, out):
    for k in range(2):
        low_high = []
        for h in range(2):
            part = []
            for i in range(2):
                pair = trade(
                    *(
                        data[16 * h : 16 * (h + 1), 4 * x + 2 * k + i].reshape(LANES, LANES)
                        for x in range(2)
                    )
                )
                part.append(
                    jnp.stack([v.reshape(16, 8, LANES) for v in pair], 1).reshape(N, LANES)
                )
            low_high.append(jnp.concatenate(part, 1))
        low, high = low_high
        for p, value in enumerate((low + high, low - high)):
            both = mul((backward[0, p], backward[1, p]), halves(value))
            for i in range(2):
                field = backward_join(both[:, LANES * i : LANES * (i + 1)])
                for s in range(8):
                    rows = pl.ds(128 * s + 32 * (2 * k + i) + p, 16, stride=2)
                    out[rows, :] = field[16 * s : 16 * (s + 1)]


def z_backward(data, table, out):
    total = 0.0
    for q in range(4):
        rows = slice(LANES * q, LANES * (q + 1))
        pair = jnp.concatenate(trade(data[2 * q], data[2 * q + 1]), 0)
        total += mul(halves(pair), (table[0, rows], table[1, rows]))
    out[...] = total * (1.0 / M**3)


def turn_green(late, green, mirror, mirror_edge, start, start_edge, zero, out):
    late = late[0] == 1
    slot = lax.broadcasted_iota(jnp.int32, (SLOTS, M), 0)
    sign = jnp.where(slot % 2 == 1, 1.0, -1.0)
    row, col = (lax.broadcasted_iota(jnp.int32, (M, M), d) for d in range(2))
    swap = jnp.where((row + col) % M == 0, 1.0, 0.0).astype(BF16)
    row, col = (lax.broadcasted_iota(jnp.int32, (LANES, HALF), d) for d in range(2))
    same = (row // HALF == col // SLOTS) & ((row + col) % SLOTS == 0)
    turn = jnp.where(same, 1.0, 0.0).astype(BF16)
    dot = functools.partial(lax.dot_general, preferred_element_type=jnp.float32)
    nn, nt = (((1,), (0,)), ((), ())), (((1,), (1,)), ((), ()))

    def rows(array, at):
        return jnp.broadcast_to(array[at : at + 1, :], (SLOTS, M))

    for k in range(8):
        owns, others = [], []
        for b in (k, 8 + k):
            mid = jnp.broadcast_to(green[SLOTS, b : b + 1, :], (SLOTS, M))
            own = jnp.where((slot == 0) & ~late, mid, green[0:SLOTS, b, :])
            owns.append(own + sign * rows(zero, b))
            if b == 0:
                other, begin, nil = mirror_edge[...], rows(start_edge, 0), rows(zero, 32)
            else:
                other, begin, nil = mirror[:, 16 - b, :], rows(start, 16 - b), rows(zero, 32 - b)
            other = jnp.where((slot == 0) & late, begin, other)
            others.append(other + sign * nil)
        own = jnp.concatenate([owns[0], owns[0], owns[1], owns[1]], 0)
        oh, ol = halves(jnp.concatenate(others, 0))
        oh, ol = halves(dot(turn, oh, nn) + dot(turn, ol, nn))
        out[k] = own.T + (dot(swap, oh, nt) + dot(swap, ol, nt))


def call(body, shape, grant, *args, scalars=0):
    vmem, smem = (pl.BlockSpec(memory_space=m) for m in (pltpu.VMEM, pltpu.SMEM))
    return pl.pallas_call(
        body,
        out_shape=jax.ShapeDtypeStruct(shape, jnp.float32),
        in_specs=[smem] * scalars + [vmem] * (len(args) - scalars),
        out_specs=vmem,
        compiler_params=pltpu.CompilerParams(vmem_limit_bytes=grant * 1024 * 1024),
        cost_estimate=pl.CostEstimate(
            flops=10**9, bytes_accessed=4 * int(np.prod(shape)), transcendentals=0
        ),
        name=body.__name__,
    )(*args)


def exchange(value, axis):
    return lax.all_to_all(value, axis, split_axis=0, concat_axis=0, tiled=True)


def reflect(value, row_shift, col_shift):
    pairs = [
        (32 * r + j, 32 * ((row_shift - r) % 8) + (col_shift - j) % 32)
        for r in range(8)
        for j in range(32)
    ]
    return lax.ppermute(value, ("row", "col"), pairs)


def spread(value):
    value = jnp.where(lax.axis_index("row") == 0, value, 0.0)
    for step in (4, 2, 1):
        pairs = [(r, r + step) for r in range(0, 8, 2 * step)]
        value = value + lax.ppermute(value, "row", pairs)
    return value


def on_device(charge, green):
    along_table, back_table, forward, backward = (jnp.asarray(t) for t in tables())
    mirror = reflect(green[SLOTS:], 7, 31)
    mirror_edge = reflect(green[SLOTS:, 0], 7, 32)
    start = reflect(green[0], 8, 31)
    start_edge = reflect(jnp.broadcast_to(green[0, :1], (8, M)), 8, 32)
    zero = spread(jnp.concatenate([green[0], start, start_edge], 0))
    late = (lax.axis_index("row") >= 4).astype(jnp.int32)[None]
    turned = call(
        turn_green, (8, M, LANES), 60, late, green, mirror, mirror_edge, start, start_edge, zero,
        scalars=1,
    )

    along_z = call(z_forward, (8, LANES, LANES), 60, charge.reshape(256, N), along_table)
    by_rows = exchange(along_z, "row").reshape(1024, LANES)
    along_y = call(y_forward, (32, 8, 8, LANES), 60, by_rows, forward)
    by_cols = exchange(along_y.reshape(32, HALF, LANES), "col").reshape(2048, LANES)
    back_x = call(x_both, (2048, LANES), 16, by_cols, turned, forward, backward)
    by_cells = exchange(back_x.reshape(32, HALF, LANES), "col")
    back_y = call(y_backward, (1024, LANES), 16, by_cells.reshape(32, 8, 8, LANES), backward)
    by_parts = exchange(back_y.reshape(8, LANES, LANES), "row")
    back_z = call(z_backward, (256, N), 16, by_parts, back_table)
    return back_z.reshape(8, 32, N)


def solution(mesh):
    in_specs = (P("col", "row", None), P("row", "col", None))
    out_specs = P("col", "row", None)
    return jax.shard_map(
        on_device, mesh=mesh, in_specs=in_specs, out_specs=out_specs, check_vma=False
    )
```

time: 179 us -> 193 us (1.078)
  blocking collectives: 94.5 us -> 63.7 us
  waiting for transfers between devices: 45.2 us -> 75.2 us
  starting transfers between devices: 13.1 us -> 30.1 us
  Pallas kernels: 23.1 us -> 18.8 us
    ppermute x0 -> x7, waiting for transfers between devices: none -> 75.2 us  [the longest x4 70.4 us: reflect(): return lax.ppermute(value, ('row', 'col'), pairs)]
    all_to_all x1, waiting for transfers between devices: 45.2 us -> 0.01 us  [exchange(): return lax.all_to_all(value, axis, split_axis=0, concat_axis=0, tiled=True)]
    all_to_all x3, blocking collectives: 94.5 us -> 63.7 us  [exchange(): return lax.all_to_all(value, axis, split_axis=0, concat_axis=0, tiled=True)]
    ppermute x0 -> x7, starting transfers between devices: none -> 17 us  [the longest x4 12.4 us: reflect(): return lax.ppermute(value, ('row', 'col'), pairs)]
    pallas_call x6, Pallas kernels: 23.1 us -> 18.8 us  [call(): pl.pallas_call(body, out_shape=jax.ShapeDtypeStruct(shape, jnp.float32),...]
  transfers between devices with their start and end apart: 1 -> 8, of which waited for: 1 -> 6; matrix products, arithmetic and copies ran while one was open for 0% -> 1% of each run, Pallas kernels for 3% -> 4%
where the time goes in v3:
time: 193 us; the launch traced here: 192 us
  waiting for transfers between devices  75.2 us (39%)
  blocking collectives  63.7 us (33%)
  starting transfers between devices  30.1 us (16%)
  Pallas kernels  18.8 us (10%)
  local copies, waits for them, and re-layouts  3.31 us (2%)
    ppermute x4, waiting for transfers between devices, reflect(): return lax.ppermute(value, ('row', 'col'), pairs)  70.4 us
    all_to_all x3, blocking collectives, exchange(): return lax.all_to_all(value, axis, split_axis=0, concat_axis=0, tiled=True)  63.7 us
    pallas_call x6, Pallas kernels, call(): pl.pallas_call(body, out_shape=jax.ShapeDtypeStruct(shape, jnp.float32),...  18.8 us
    all_to_all x1, starting transfers between devices, exchange(): return lax.all_to_all(value, axis, split_axis=0, concat_axis=0, tiled=True)  13.1 us
    ppermute x4, starting transfers between devices, reflect(): return lax.ppermute(value, ('row', 'col'), pairs)  12.4 us
    ppermute x3, waiting for transfers between devices, spread(): value = value + lax.ppermute(value, 'row', pairs)  4.75 us
    ppermute x3, starting transfers between devices, spread(): value = value + lax.ppermute(value, 'row', pairs)  4.59 us
  transfers between devices with their start and end apart: 8, of which 6 were waited for; matrix products, arithmetic and copies ran while one was open for 1% of the time, Pallas kernels for 4%

profile of v3, /device:TPU:1, one launch (start us, length us, event | category | flops | bytes accessed | tf_op | source)
XLA Modules:
  0.0 191.9 jit_solution(9353956837872381348)
XLA Ops:
  0.0 2.6 %z_forward.1 = f32[8,128,128]{2,1,0:T(8,128)} custom-call(f32[256,256]{1,0:T(8,128)} %bitcast.23, bf16[2,512,256]{2,1,0:T(8,128)(2,1)} %constant.20.clone.table), custom_call_target="tpu_custom_call" | custom-call | flops 1000000000 | bytes 524288 | tf_op jit(solution)/shard_map/z_forward/pallas_call | solution.py:210
  2.6 14.9 %all_to_all.20 = f32[8,128,128]{2,1,0:T(8,128)} all-to-all(f32[8,128,128]{2,1,0:T(8,128)} %z_forward.1), channel_id=1, replica_groups=mesh['row'=8,'col'=32] {'row'}, dimensions={0} | all-to-all | bytes 1048576 | tf_op jit(solution)/shard_map/all_to_all | solution.py:224
  17.5 0.0 copy-start.4
  17.5 3.2 %y_forward.1 = f32[32,8,8,128]{3,2,1,0:T(8,128)} custom-call(f32[1024,128]{1,0:T(8,128)} %bitcast.20, bf16[2,2,256,256]{3,2,1,0:T(8,128)(2,1)} %constant.22.clone.table.forward), custom_call_target="tpu_custom_call" | custom-call | flops 1000000000 | bytes 1048576 | tf_op jit(solution)/shard_map/y_forward/pallas_call | solution.py:210
  20.7 13.1 %all-to-all-start.1 = ((f32[32,64,128]{2,1,0:T(8,128)}), f32[32,64,128]{2,1,0:T(8,128)S(1)}, u32[]{:S(2)}, u32[]{:S(2)}) async-start(f32[32,64,128]{2,1,0:T(8,128)} %bitcast.19), calls=%async_computation.1 | async-start | bytes 2097152 | tf_op jit(solution)/shard_map/all_to_all | solution.py:224
  33.7 0.0 copy-done.4
  33.7 1.1 slice.13
  34.8 5.3 %collective-permute-start = (f32[32,16,512]{2,1,0:T(8,128)}, f32[32,16,512]{2,1,0:T(8,128)}, u32[]{:S(2)}, u32[]{:S(2)}) collective-permute-start(f32[32,16,512]{2,1,0:T(8,128)} %slice.13), channel_id=1, source_target_pairs={{0,255},{1,254},{2,253},{3,252},{4,251},{5,250},{6,249},{7,248},{8... | collective-permute-start | bytes 3145736 | tf_op jit(solution)/shard_map/ppermute | solution.py:233
  40.1 0.0 collective-permute-start.2
  40.1 7.0 %collective-permute-start.3 = (f32[8,512]{1,0:T(8,128)S(1)}, f32[8,512]{1,0:T(8,128)S(1)}, u32[]{:S(2)}, u32[]{:S(2)}) collective-permute-start(f32[8,512]{1,0:T(8,128)S(1)} %broadcast_in_dim.19), channel_id=1, source_target_pairs={{0,0},{1,31},{2,30},{3,29},{4,28},{5,27},{6,26},{7,25},{8,24},{9,2... | collective-permute-start | bytes 49160 | tf_op jit(solution)/shard_map/ppermute | solution.py:233
  47.1 63.0 %collective-permute-done.3.start_edge = f32[8,512]{1,0:T(8,128)S(1)} collective-permute-done((f32[8,512]{1,0:T(8,128)S(1)}, f32[8,512]{1,0:T(8,128)S(1)}, u32[]{:S(2)}, u32[]{:S(2)}) %collective-permute-start.3) | collective-permute-done | bytes 16416 | tf_op jit(solution)/shard_map/ppermute | solution.py:233
  110.2 0.0 copy-start.7
  110.2 0.4 collective-permute-done.2.start
  110.6 0.0 copy-start.5
  110.6 2.0 %collective-permute-start.4 = (f32[40,512]{1,0:T(8,128)S(1)}, f32[40,512]{1,0:T(8,128)S(1)}, u32[]{:S(2)}, u32[]{:S(2)}) collective-permute-start(f32[40,512]{1,0:T(8,128)S(1)} %maximum_select_fusion), channel_id=1, source_target_pairs={{0,128},{1,129},{2,130},{3,131},{4,132},{5,133},{6,134},{7,135},{8... | collective-permute-start | bytes 245768 | tf_op jit(solution)/shard_map/ppermute | solution.py:240
  112.6 2.0 %collective-permute-done.4 = f32[40,512]{1,0:T(8,128)S(1)} collective-permute-done((f32[40,512]{1,0:T(8,128)S(1)}, f32[40,512]{1,0:T(8,128)S(1)}, u32[]{:S(2)}, u32[]{:S(2)}) %collective-permute-start.4) | collective-permute-done | bytes 81952 | tf_op jit(solution)/shard_map/ppermute | solution.py:240
  114.6 1.3 collective-permute-start.5
  115.9 1.5 collective-permute-done.5
  117.4 1.3 collective-permute-start.6
  118.8 0.1 collective-permute-start.1
  118.9 1.3 collective-permute-done.6
  120.2 0.6 add.11.zero
  120.8 7.0 %collective-permute-done.1.mirror_edge = f32[32,512]{1,0:T(8,128)S(1)} collective-permute-done((f32[32,512]{1,0:T(8,128)S(1)}, f32[32,512]{1,0:T(8,128)S(1)}, u32[]{:S(2)}, u32[]{:S(2)}) %collective-permute-start.1) | collective-permute-done | bytes 65568 | tf_op jit(solution)/shard_map/ppermute | solution.py:233
  127.8 0.0 copy-start.6
  127.8 0.0 collective-permute-done.mirror
  127.8 0.0 copy-done.7
  127.8 0.0 copy-done.5
  127.8 0.6 copy-done.6
  128.4 0.0 copy-start.1
  128.4 0.0 copy-start.2
  128.4 7.4 %turn_green.1.green = f32[8,512,128]{2,1,0:T(8,128)} custom-call(s32[1]{0:T(128)} %bitcast.4.late, f32[64,16,512]{2,1,0:T(8,128)} %green.1, f32[32,16,512]{2,1,0:T(8,128)} %collective-permute-done.mirror, f32[32,512]{1,0:T(8,128)} %copy-done.6, f32[16,512]{1,0:T(8,128)} %copy-done.5, f32[8,512]{1,0:T(8,128)} %copy-done.7, f32[40,512]{1,0:T(8,128)} %add.11.zero), custom_call_target="tpu_custom_call" | custom-call | flops 1000000000 | bytes 2097152 | tf_op jit(solution)/shard_map/turn_green/pallas_call | solution.py:210
  135.9 0.0 all-to-all-done.1
  135.9 0.0 copy-done.1
  135.9 0.0 copy-done.2
  135.9 0.0 copy-start
  135.9 1.6 copy-done
  137.5 3.3 %x_both.1 = f32[2048,128]{1,0:T(8,128)S(1)} custom-call(f32[2048,128]{1,0:T(8,128)S(1)} %bitcast.15, f32[8,512,128]{2,1,0:T(8,128)S(1)} %copy-done, bf16[2,2,256,256]{3,2,1,0:T(8,128)(2,1)S(1)} %copy-done.2, bf16[2,2,256,256]{3,2,1,0:T(8,128)(2,1)S(1)} %copy-done.1), custom_call_target="tpu_custom_call" | custom-call | flops 1000000000 | bytes 1048576 | tf_op jit(solution)/shard_map/x_both/pallas_call | solution.py:210
  140.8 34.4 %all_to_all.21 = f32[32,64,128]{2,1,0:T(8,128)S(1)} all-to-all(f32[32,64,128]{2,1,0:T(8,128)S(1)} %bitcast.16), channel_id=1, replica_groups=mesh['row'=8,'col'=32] {'col'}, dimensions={0} | all-to-all | bytes 2097152 | tf_op jit(solution)/shard_map/all_to_all | solution.py:224
  175.2 0.0 copy-start.3
  175.2 0.9 y_backward.1
  176.1 14.4 %all_to_all.22.data = f32[8,128,128]{2,1,0:T(8,128)S(1)} all-to-all(f32[8,128,128]{2,1,0:T(8,128)S(1)} %bitcast.18), channel_id=1, replica_groups=mesh['row'=8,'col'=32] {'row'}, dimensions={0} | all-to-all | bytes 1048576 | tf_op jit(solution)/shard_map/all_to_all | solution.py:224
  190.5 0.0 copy-done.3
  190.5 1.3 z_backward.1
  (8 shorter events, 0.1 us)
Async XLA Ops:
  17.5 16.3 %copy-start.4 = (f32[64,16,512]{2,1,0:T(8,128)S(1)}, f32[64,16,512]{2,1,0:T(8,128)}, u32[]{:S(2)}) copy-start(f32[64,16,512]{2,1,0:T(8,128)} %green.1) | copy-start | bytes 6291460
  20.7 115.2 %all-to-all-start.1 = ((f32[32,64,128]{2,1,0:T(8,128)}), f32[32,64,128]{2,1,0:T(8,128)S(1)}, u32[]{:S(2)}, u32[]{:S(2)}) async-start(f32[32,64,128]{2,1,0:T(8,128)} %bitcast.19), calls=%async_computation.1 | async-start | bytes 2097152 | tf_op jit(solution)/shard_map/all_to_all | solution.py:224
  34.8 93.0 %collective-permute-start = (f32[32,16,512]{2,1,0:T(8,128)}, f32[32,16,512]{2,1,0:T(8,128)}, u32[]{:S(2)}, u32[]{:S(2)}) collective-permute-start(f32[32,16,512]{2,1,0:T(8,128)} %slice.13), channel_id=1, source_target_pairs={{0,255},{1,254},{2,253},{3,252},{4,251},{5,250},{6,249},{7,248},{8... | collective-permute-start | bytes 3145736 | tf_op jit(solution)/shard_map/ppermute | solution.py:233
  40.1 70.5 %collective-permute-start.2 = (f32[16,512]{1,0:T(8,128)S(1)}, f32[16,512]{1,0:T(8,128)S(1)}, u32[]{:S(2)}, u32[]{:S(2)}) collective-permute-start(f32[16,512]{1,0:T(8,128)S(1)} %slice_bitcast_fusion), channel_id=1, source_target_pairs={{0,31},{1,30},{2,29},{3,28},{4,27},{5,26},{6,25},{7,24},{8,23},{9,... | collective-permute-start | bytes 98312 | tf_op jit(solution)/shard_map/ppermute | solution.py:233
  40.1 70.0 %collective-permute-start.3 = (f32[8,512]{1,0:T(8,128)S(1)}, f32[8,512]{1,0:T(8,128)S(1)}, u32[]{:S(2)}, u32[]{:S(2)}) collective-permute-start(f32[8,512]{1,0:T(8,128)S(1)} %broadcast_in_dim.19), channel_id=1, source_target_pairs={{0,0},{1,31},{2,30},{3,29},{4,28},{5,27},{6,26},{7,25},{8,24},{9,2... | collective-permute-start | bytes 49160 | tf_op jit(solution)/shard_map/ppermute | solution.py:233
  110.2 17.6 %copy-start.7 = (f32[8,512]{1,0:T(8,128)}, f32[8,512]{1,0:T(8,128)S(1)}, u32[]{:S(2)}) copy-start(f32[8,512]{1,0:T(8,128)S(1)} %collective-permute-done.3.start_edge) | copy-start | bytes 49156
  110.6 17.2 %copy-start.5 = (f32[16,512]{1,0:T(8,128)}, f32[16,512]{1,0:T(8,128)S(1)}, u32[]{:S(2)}) copy-start(f32[16,512]{1,0:T(8,128)S(1)} %collective-permute-done.2.start) | copy-start | bytes 98308
  110.6 4.0 %collective-permute-start.4 = (f32[40,512]{1,0:T(8,128)S(1)}, f32[40,512]{1,0:T(8,128)S(1)}, u32[]{:S(2)}, u32[]{:S(2)}) collective-permute-start(f32[40,512]{1,0:T(8,128)S(1)} %maximum_select_fusion), channel_id=1, source_target_pairs={{0,128},{1,129},{2,130},{3,131},{4,132},{5,133},{6,134},{7,135},{8... | collective-permute-start | bytes 245768 | tf_op jit(solution)/shard_map/ppermute | solution.py:240
  114.6 2.8 %collective-permute-start.5 = (f32[40,512]{1,0:T(8,128)S(1)}, f32[40,512]{1,0:T(8,128)S(1)}, u32[]{:S(2)}, u32[]{:S(2)}) collective-permute-start(f32[40,512]{1,0:T(8,128)S(1)} %add.9), channel_id=1, source_target_pairs={{0,64},{128,192},{1,65},{129,193},{2,66},{130,194},{3,67},{131,195... | collective-permute-start | bytes 245768 | tf_op jit(solution)/shard_map/ppermute | solution.py:240
  117.4 2.8 %collective-permute-start.6 = (f32[40,512]{1,0:T(8,128)S(1)}, f32[40,512]{1,0:T(8,128)S(1)}, u32[]{:S(2)}, u32[]{:S(2)}) collective-permute-start(f32[40,512]{1,0:T(8,128)S(1)} %add.10), channel_id=1, source_target_pairs={{0,32},{64,96},{128,160},{192,224},{1,33},{65,97},{129,161},{193,2... | collective-permute-start | bytes 245768 | tf_op jit(solution)/shard_map/ppermute | solution.py:240
  118.8 9.0 %collective-permute-start.1 = (f32[32,512]{1,0:T(8,128)S(1)}, f32[32,512]{1,0:T(8,128)S(1)}, u32[]{:S(2)}, u32[]{:S(2)}) collective-permute-start(f32[32,512]{1,0:T(8,128)S(1)} %bitcast.21), channel_id=1, source_target_pairs={{0,224},{1,255},{2,254},{3,253},{4,252},{5,251},{6,250},{7,249},{8... | collective-permute-start | bytes 196616 | tf_op jit(solution)/shard_map/ppermute | solution.py:233
  127.8 0.6 copy-start.6
  128.4 7.5 %copy-start.1 = (bf16[2,2,256,256]{3,2,1,0:T(8,128)(2,1)S(1)}, bf16[2,2,256,256]{3,2,1,0:T(8,128)(2,1)}, u32[]{:S(2)}) copy-start(bf16[2,2,256,256]{3,2,1,0:T(8,128)(2,1)} %constant.23.clone.backward) | copy-start | bytes 1572868
  128.4 7.5 %copy-start.2 = (bf16[2,2,256,256]{3,2,1,0:T(8,128)(2,1)S(1)}, bf16[2,2,256,256]{3,2,1,0:T(8,128)(2,1)}, u32[]{:S(2)}) copy-start(bf16[2,2,256,256]{3,2,1,0:T(8,128)(2,1)} %constant.22.clone.table.forward) | copy-start | bytes 1572868
  135.9 1.6 copy-start
  175.2 15.3 %copy-start.3 = (bf16[2,512,256]{2,1,0:T(8,128)(2,1)S(1)}, bf16[2,512,256]{2,1,0:T(8,128)(2,1)}, u32[]{:S(2)}) copy-start(bf16[2,512,256]{2,1,0:T(8,128)(2,1)} %constant.21.clone.table) | copy-start | bytes 1572868

commit v4 on v3

--- a/solution.py
+++ b/solution.py
@@ -8,6 +8,7 @@
 from jax.experimental import pallas as pl
 from jax.experimental.pallas import tpu as pltpu
 from jax.sharding import PartitionSpec as P
+
 
 M = 512
 N = 256
@@ -35,11 +36,9 @@
     freq = np.arange(8)[:, None] * HALF + np.arange(SLOTS)[None, :]
     freq[:4, 0] += SLOTS
     angle = 2.0 * np.pi * ((freq[:, :, None] * np.arange(N)) % M) / M
-    back_z = np.concatenate([np.cos(angle), -np.sin(angle)], 1).reshape(M, N)
-    own = np.concatenate([freq == N, freq == N], 1).reshape(M, 1)
-    along_z = np.where(own, 0.5, 1.0) * back_z
+    along_z = np.concatenate([np.cos(angle), -np.sin(angle)], 1).reshape(M, N)
     return tuple(
-        np.stack(split_table(t)) for t in (along_z, back_z, forward, forward.transpose(0, 2, 1))
+        np.stack(split_table(t)) for t in (along_z, forward, forward.transpose(0, 2, 1))
     )
 
 
@@ -94,7 +93,7 @@
     ]
 
 
-def y_forward(data, table, out):
+def y_forward(data, table, out, held):
     for k in range(2):
         cols = [
             [
@@ -109,35 +108,14 @@
         for i in range(2):
             at = slice(LANES * i, LANES * (i + 1))
             for h, value in enumerate((even[:, at] + odd[:, at], even[:, at] - odd[:, at])):
-                value = value.reshape(16, 2, 8, LANES)
-                pair = trade(value[:, 0].reshape(LANES, LANES), value[:, 1].reshape(LANES, LANES))
+                at_b = N * (2 * i + h)
+                held[pl.ds(at_b, N), :] = value
+                pair = trade(*(held[pl.ds(at_b + t, LANES, stride=2), :] for t in range(2)))
                 for x in range(2):
                     out[16 * h : 16 * (h + 1), 4 * x + 2 * k + i] = pair[x].reshape(16, 8, LANES)
 
 
-def x_both(data, green, forward, backward, out):
-    def step(k, carry):
-        cols = [
-            [data[pl.ds(8 * p + 2 * k + i, LANES, stride=16), :] for i in range(2)]
-            for p in range(2)
-        ]
-        even, odd = both_parities(forward, cols)
-        low, high = (
-            jnp.concatenate([green[2 * k + i, N * h : N * (h + 1)] for i in range(2)], 1)
-            for h in range(2)
-        )
-        low, high = (even + odd) * low, (even - odd) * high
-        for p, value in enumerate((low + high, low - high)):
-            both = mul((backward[0, p], backward[1, p]), halves(value))
-            for i in range(2):
-                field = backward_join(both[:, LANES * i : LANES * (i + 1)])
-                out[pl.ds(8 * p + 2 * k + i, LANES, stride=16), :] = field
-        return carry
-
-    lax.fori_loop(0, 4, step, 0, unroll=2)
-
-
-def y_backward(data, backward, out):
+def y_backward(data, backward, out, held):
     for k in range(2):
         low_high = []
         for h in range(2):
@@ -149,9 +127,10 @@
                         for x in range(2)
                     )
                 )
-                part.append(
-                    jnp.stack([v.reshape(16, 8, LANES) for v in pair], 1).reshape(N, LANES)
-                )
+                at_b = N * (2 * i + h)
+                for t in range(2):
+                    held[pl.ds(at_b + t, LANES, stride=2), :] = pair[t]
+                part.append(held[pl.ds(at_b, N), :])
             low_high.append(jnp.concatenate(part, 1))
         low, high = low_high
         for p, value in enumerate((low + high, low - high)):
@@ -172,10 +151,11 @@
     out[...] = total * (1.0 / M**3)
 
 
-def turn_green(late, green, mirror, mirror_edge, start, start_edge, zero, out):
-    late = late[0] == 1
+def turn_green(up, late, green, middle, mirror, mirror_up, mirror_edge, start, start_edge, zero, out):
+    late, own_mirror = late[0] > 0, late[0] > 1
     slot = lax.broadcasted_iota(jnp.int32, (SLOTS, M), 0)
     sign = jnp.where(slot % 2 == 1, 1.0, -1.0)
+    share = jnp.where((slot == 0) & own_mirror, 0.5, 1.0)
     row, col = (lax.broadcasted_iota(jnp.int32, (M, M), d) for d in range(2))
     swap = jnp.where((row + col) % M == 0, 1.0, 0.0).astype(BF16)
     row, col = (lax.broadcasted_iota(jnp.int32, (LANES, HALF), d) for d in range(2))
@@ -187,37 +167,78 @@
     def rows(array, at):
         return jnp.broadcast_to(array[at : at + 1, :], (SLOTS, M))
 
-    for k in range(8):
+    for k in range(4):
         owns, others = [], []
-        for b in (k, 8 + k):
-            mid = jnp.broadcast_to(green[SLOTS, b : b + 1, :], (SLOTS, M))
-            own = jnp.where((slot == 0) & ~late, mid, green[0:SLOTS, b, :])
-            owns.append(own + sign * rows(zero, b))
+        for b in (8 * up + 2 * k, 8 * up + 2 * k + 1):
+            at = b - 8 * up
+            mid = jnp.broadcast_to(middle[0, at : at + 1, :], (SLOTS, M))
+            own = jnp.where((slot == 0) & ~late, mid, green[:, at, :])
+            owns.append((own + sign * rows(zero, b)) * share)
             if b == 0:
                 other, begin, nil = mirror_edge[...], rows(start_edge, 0), rows(zero, 32)
             else:
-                other, begin, nil = mirror[:, 16 - b, :], rows(start, 16 - b), rows(zero, 32 - b)
+                other = mirror[:, 8 - b, :] if b <= 8 else mirror_up[:, 16 - b, :]
+                begin, nil = rows(start, 16 - b), rows(zero, 32 - b)
             other = jnp.where((slot == 0) & late, begin, other)
-            others.append(other + sign * nil)
+            others.append((other + sign * nil) * share)
         own = jnp.concatenate([owns[0], owns[0], owns[1], owns[1]], 0)
         oh, ol = halves(jnp.concatenate(others, 0))
         oh, ol = halves(dot(turn, oh, nn) + dot(turn, ol, nn))
         out[k] = own.T + (dot(swap, oh, nt) + dot(swap, ol, nt))
 
 
-def call(body, shape, grant, *args, scalars=0):
+def turn_first(late, green, middle, mirror, mirror_edge, start, start_edge, zero, out):
+    turn_green(0, late, green, middle, mirror, None, mirror_edge, start, start_edge, zero, out)
+
+
+def x_both(
+    late, green, middle, data, turned, mirror, mirror_up, start, zero, forward, backward, out, turned_up
+):
+    turn_green(1, late, green, middle, mirror, mirror_up, None, start, None, zero, turned_up)
+
+    def step(own, at, k):
+        k = at + 2 * k
+        cols = [
+            [data[pl.ds(8 * p + k + i, LANES, stride=16), :] for i in range(2)] for p in range(2)
+        ]
+        even, odd = both_parities(forward, cols)
+        low, high = (
+            jnp.concatenate([own[k - at + i, N * h : N * (h + 1)] for i in range(2)], 1)
+            for h in range(2)
+        )
+        low, high = (even + odd) * low, (even - odd) * high
+        for p, value in enumerate((low + high, low - high)):
+            both = mul((backward[0, p], backward[1, p]), halves(value))
+            for i in range(2):
+                field = backward_join(both[:, LANES * i : LANES * (i + 1)])
+                out[pl.ds(8 * p + k + i, LANES, stride=16), :] = field
+
+    for at, own in ((0, turned), (4, turned_up)):
+        for k in range(2):
+            step(own, at, k)
+
+
+def call(body, shape, grant, *args, scalars=0, scratch=(), blocks=()):
     vmem, smem = (pl.BlockSpec(memory_space=m) for m in (pltpu.VMEM, pltpu.SMEM))
     return pl.pallas_call(
         body,
         out_shape=jax.ShapeDtypeStruct(shape, jnp.float32),
-        in_specs=[smem] * scalars + [vmem] * (len(args) - scalars),
+        grid=(1,) if blocks else (),
+        in_specs=[smem] * scalars + [*blocks] + [vmem] * (len(args) - scalars - len(blocks)),
         out_specs=vmem,
+        scratch_shapes=[pltpu.VMEM(s, jnp.float32) for s in scratch],
         compiler_params=pltpu.CompilerParams(vmem_limit_bytes=grant * 1024 * 1024),
         cost_estimate=pl.CostEstimate(
             flops=10**9, bytes_accessed=4 * int(np.prod(shape)), transcendentals=0
         ),
-        name=body.__name__,
     )(*args)
+
+
+def green_blocks(up):
+    return [
+        pl.BlockSpec((SLOTS, 8, M), lambda i: (0, up, 0)),
+        pl.BlockSpec((1, 8, M), lambda i: (SLOTS, up, 0)),
+    ]
 
 
 def exchange(value, axis):
@@ -242,27 +263,42 @@
 
 
 def on_device(charge, green):
-    along_table, back_table, forward, backward = (jnp.asarray(t) for t in tables())
-    mirror = reflect(green[SLOTS:], 7, 31)
+    z_table, forward, backward = (jnp.asarray(t) for t in tables())
+    moves = {
+        "mirror": ("col", [(j, j ^ 29) for j in range(32)]),
+        "across": (("row", "col"), [(i, i ^ 226) for i in range(256)]),
+    }
+    mirrors = []
+    for k, order in enumerate((("mirror", "across"), ("across", "mirror"))):
+        half = green[SLOTS:, 8 * (1 - k) : 8 * (2 - k)]
+        for name in order:
+            half = lax.ppermute(half, *moves[name])
+        mirrors.append(half)
     mirror_edge = reflect(green[SLOTS:, 0], 7, 32)
     start = reflect(green[0], 8, 31)
     start_edge = reflect(jnp.broadcast_to(green[0, :1], (8, M)), 8, 32)
     zero = spread(jnp.concatenate([green[0], start, start_edge], 0))
-    late = (lax.axis_index("row") >= 4).astype(jnp.int32)[None]
+    row = lax.axis_index("row")
+    late = ((row >= 4).astype(jnp.int32) + (row == 4).astype(jnp.int32))[None]
     turned = call(
-        turn_green, (8, M, LANES), 60, late, green, mirror, mirror_edge, start, start_edge, zero,
-        scalars=1,
-    )
-
-    along_z = call(z_forward, (8, LANES, LANES), 60, charge.reshape(256, N), along_table)
+        turn_first, (4, M, LANES), 60, late, green, green, mirrors[0], mirror_edge, start, start_edge,
+        zero, scalars=1, blocks=green_blocks(0),
+    )
+    along_z = call(z_forward, (8, LANES, LANES), 60, charge.reshape(256, N), z_table)
     by_rows = exchange(along_z, "row").reshape(1024, LANES)
-    along_y = call(y_forward, (32, 8, 8, LANES), 60, by_rows, forward)
+    along_y = call(y_forward, (32, 8, 8, LANES), 60, by_rows, forward, scratch=[(2 * M, LANES)])
     by_cols = exchange(along_y.reshape(32, HALF, LANES), "col").reshape(2048, LANES)
-    back_x = call(x_both, (2048, LANES), 16, by_cols, turned, forward, backward)
+    back_x = call(
+        x_both, (2048, LANES), 60, late, green, green, by_cols, turned, *mirrors, start, zero,
+        forward, backward, scalars=1, blocks=green_blocks(1), scratch=[(4, M, LANES)],
+    )
     by_cells = exchange(back_x.reshape(32, HALF, LANES), "col")
-    back_y = call(y_backward, (1024, LANES), 16, by_cells.reshape(32, 8, 8, LANES), backward)
+    back_y = call(
+        y_backward, (1024, LANES), 16, by_cells.reshape(32, 8, 8, LANES), backward,
+        scratch=[(2 * M, LANES)],
+    )
     by_parts = exchange(back_y.reshape(8, LANES, LANES), "row")
-    back_z = call(z_backward, (256, N), 16, by_parts, back_table)
+    back_z = call(z_backward, (256, N), 16, by_parts, z_table)
     return back_z.reshape(8, 32, N)
 
 

time: 193 us -> 196 us (1.016)
  starting transfers between devices: 30.1 us -> 38.2 us
  waiting for transfers between devices: 75.2 us -> 68.9 us
    ppermute x4 -> x3, waiting for transfers between devices: 70.4 us -> 13.6 us  [reflect(): return lax.ppermute(value, ('row', 'col'), pairs)]
    ppermute x0 -> x4, waiting for transfers between devices: none -> 50 us  [on_device(): half = lax.ppermute(half, *moves[name])]
    ppermute x0 -> x4, starting transfers between devices: none -> 14.5 us  [on_device(): half = lax.ppermute(half, *moves[name])]
    ppermute x4 -> x3, starting transfers between devices: 12.4 us -> 6.49 us  [reflect(): return lax.ppermute(value, ('row', 'col'), pairs)]
  transfers between devices with their start and end apart: 8 -> 11, of which waited for: 6 -> 8; matrix products, arithmetic and copies ran while one was open for 1% -> 0% of each run, Pallas kernels for 4% -> 2%
where the time goes in v4:
time: 196 us; the launch traced here: 194 us
  waiting for transfers between devices  68.9 us (35%)
  blocking collectives  63.7 us (32%)
  starting transfers between devices  38.2 us (19%)
  Pallas kernels  20.6 us (11%)
    all_to_all x3, blocking collectives, exchange(): return lax.all_to_all(value, axis, split_axis=0, concat_axis=0, tiled=True)  63.7 us
    ppermute x4, waiting for transfers between devices, on_device(): half = lax.ppermute(half, *moves[name])  50 us
    pallas_call x6, Pallas kernels, call(): pl.pallas_call(body, out_shape=jax.ShapeDtypeStruct(shape, jnp.float32),...  20.6 us
    ppermute x4, starting transfers between devices, on_device(): half = lax.ppermute(half, *moves[name])  14.5 us
    ppermute x3, waiting for transfers between devices, reflect(): return lax.ppermute(value, ('row', 'col'), pairs)  13.6 us
    all_to_all x1, starting transfers between devices, exchange(): return lax.all_to_all(value, axis, split_axis=0, concat_axis=0, tiled=True)  13.1 us
    ppermute x3, starting transfers between devices, reflect(): return lax.ppermute(value, ('row', 'col'), pairs)  6.49 us
    ppermute x3, waiting for transfers between devices, spread(): value = value + lax.ppermute(value, 'row', pairs)  5.32 us
  transfers between devices with their start and end apart: 11, of which 8 were waited for; matrix products, arithmetic and copies ran while one was open for 0% of the time, Pallas kernels for 2%

profile of v4, /device:TPU:1, one launch (start us, length us, event | category | flops | bytes accessed | tf_op | source)
XLA Modules:
  0.0 193.9 jit_solution(17926042294461099103)
XLA Ops:
  0.0 2.6 %shard_map.55 = f32[8,128,128]{2,1,0:T(8,128)} custom-call(f32[256,256]{1,0:T(8,128)} %bitcast.23, bf16[2,512,256]{2,1,0:T(8,128)(2,1)} %constant.18.clone.table), custom_call_target="tpu_custom_call" | custom-call | flops 1000000000 | bytes 524288 | tf_op jit(solution)/shard_map/pallas_call | solution.py:223
  2.6 14.9 %all_to_all.20 = f32[8,128,128]{2,1,0:T(8,128)} all-to-all(f32[8,128,128]{2,1,0:T(8,128)} %shard_map.55), channel_id=1, replica_groups=mesh['row'=8,'col'=32] {'row'}, dimensions={0} | all-to-all | bytes 1048576 | tf_op jit(solution)/shard_map/all_to_all | solution.py:245
  17.5 0.0 copy-start.2
  17.5 3.2 %shard_map.56 = f32[32,8,8,128]{3,2,1,0:T(8,128)} custom-call(f32[1024,128]{1,0:T(8,128)} %bitcast.20, bf16[2,2,256,256]{3,2,1,0:T(8,128)(2,1)} %constant.19.clone.table.forward), custom_call_target="tpu_custom_call" | custom-call | flops 1000000000 | bytes 1048576 | tf_op jit(solution)/shard_map/pallas_call | solution.py:223
  20.7 13.1 %all-to-all-start.1 = ((f32[32,64,128]{2,1,0:T(8,128)}), f32[32,64,128]{2,1,0:T(8,128)S(1)}, u32[]{:S(2)}, u32[]{:S(2)}) async-start(f32[32,64,128]{2,1,0:T(8,128)} %bitcast.19), calls=%async_computation.1 | async-start | bytes 2097152 | tf_op jit(solution)/shard_map/all_to_all | solution.py:245
  33.8 0.0 copy-done.2
  33.8 0.1 fusion
  33.9 2.9 %collective-permute-start.8 = (f32[32,8,512]{2,1,0:T(8,128)S(1)}, f32[32,8,512]{2,1,0:T(8,128)}, u32[]{:S(2)}, u32[]{:S(2)}) collective-permute-start(f32[32,8,512]{2,1,0:T(8,128)S(1)} %get-tuple-element.5), channel_id=1, source_target_pairs={{0,226},{1,227},{2,224},{3,225},{4,230},{5,231},{6,228},{7,229},{8... | collective-permute-start | bytes 1572872 | tf_op jit(solution)/shard_map/ppermute | solution.py:275
  36.8 3.0 %collective-permute-start = (f32[32,8,512]{2,1,0:T(8,128)S(1)}, f32[32,8,512]{2,1,0:T(8,128)}, u32[]{:S(2)}, u32[]{:S(2)}) collective-permute-start(f32[32,8,512]{2,1,0:T(8,128)S(1)} %get-tuple-element.6), channel_id=1, source_target_pairs={{0,29},{1,28},{2,31},{3,30},{4,25},{5,24},{6,27},{7,26},{8,21},{9,... | collective-permute-start | bytes 1572872 | tf_op jit(solution)/shard_map/ppermute | solution.py:275
  39.8 17.1 %collective-permute-done.8 = f32[32,8,512]{2,1,0:T(8,128)} collective-permute-done((f32[32,8,512]{2,1,0:T(8,128)S(1)}, f32[32,8,512]{2,1,0:T(8,128)}, u32[]{:S(2)}, u32[]{:S(2)}) %collective-permute-start.8) | collective-permute-done | bytes 524320 | tf_op jit(solution)/shard_map/ppermute | solution.py:275
  56.9 5.8 %collective-permute-start.9 = (f32[32,8,512]{2,1,0:T(8,128)}, f32[32,8,512]{2,1,0:T(8,128)}, u32[]{:S(2)}, u32[]{:S(2)}) collective-permute-start(f32[32,8,512]{2,1,0:T(8,128)} %collective-permute-done.8), channel_id=1, source_target_pairs={{0,29},{1,28},{2,31},{3,30},{4,25},{5,24},{6,27},{7,26},{8,21},{9,... | collective-permute-start | bytes 1572872 | tf_op jit(solution)/shard_map/ppermute | solution.py:275
  62.7 32.9 %collective-permute-done = f32[32,8,512]{2,1,0:T(8,128)} collective-permute-done((f32[32,8,512]{2,1,0:T(8,128)S(1)}, f32[32,8,512]{2,1,0:T(8,128)}, u32[]{:S(2)}, u32[]{:S(2)}) %collective-permute-start) | collective-permute-done | bytes 524320 | tf_op jit(solution)/shard_map/ppermute | solution.py:275
  95.6 2.7 %collective-permute-start.1 = (f32[32,8,512]{2,1,0:T(8,128)}, f32[32,8,512]{2,1,0:T(8,128)}, u32[]{:S(2)}, u32[]{:S(2)}) collective-permute-start(f32[32,8,512]{2,1,0:T(8,128)} %collective-permute-done), channel_id=1, source_target_pairs={{0,226},{1,227},{2,224},{3,225},{4,230},{5,231},{6,228},{7,229},{8... | collective-permute-start | bytes 1572872 | tf_op jit(solution)/shard_map/ppermute | solution.py:275
  98.3 0.0 collective-permute-start.3
  98.4 6.4 %collective-permute-start.4 = (f32[8,512]{1,0:T(8,128)S(1)}, f32[8,512]{1,0:T(8,128)S(1)}, u32[]{:S(2)}, u32[]{:S(2)}) collective-permute-start(f32[8,512]{1,0:T(8,128)S(1)} %broadcast_in_dim.16), channel_id=1, source_target_pairs={{0,0},{1,31},{2,30},{3,29},{4,28},{5,27},{6,26},{7,25},{8,24},{9,2... | collective-permute-start | bytes 49160 | tf_op jit(solution)/shard_map/ppermute | solution.py:254
  104.8 6.0 %collective-permute-done.4.start_edge = f32[8,512]{1,0:T(8,128)S(1)} collective-permute-done((f32[8,512]{1,0:T(8,128)S(1)}, f32[8,512]{1,0:T(8,128)S(1)}, u32[]{:S(2)}, u32[]{:S(2)}) %collective-permute-start.4) | collective-permute-done | bytes 16416 | tf_op jit(solution)/shard_map/ppermute | solution.py:254
  110.7 0.0 copy-start.6
  110.7 0.7 collective-permute-done.3.start
  111.5 0.0 copy-start.4
  111.5 1.6 collective-permute-start.5
  113.1 2.2 %collective-permute-done.5 = f32[40,512]{1,0:T(8,128)S(1)} collective-permute-done((f32[40,512]{1,0:T(8,128)S(1)}, f32[40,512]{1,0:T(8,128)S(1)}, u32[]{:S(2)}, u32[]{:S(2)}) %collective-permute-start.5) | collective-permute-done | bytes 81952 | tf_op jit(solution)/shard_map/ppermute | solution.py:261
  115.3 1.3 collective-permute-start.6
  116.6 1.8 collective-permute-done.6
  118.4 1.3 collective-permute-start.7
  119.8 0.1 collective-permute-start.2
  119.9 1.3 collective-permute-done.7
  121.2 0.6 add.15.zero
  121.8 6.9 %collective-permute-done.2.mirror_edge = f32[32,512]{1,0:T(8,128)S(1)} collective-permute-done((f32[32,512]{1,0:T(8,128)S(1)}, f32[32,512]{1,0:T(8,128)S(1)}, u32[]{:S(2)}, u32[]{:S(2)}) %collective-permute-start.2) | collective-permute-done | bytes 65568 | tf_op jit(solution)/shard_map/ppermute | solution.py:254
  128.7 0.0 copy-start.5
  128.7 0.0 collective-permute-done.1.mirror
  128.7 0.0 copy-done.6
  128.7 0.0 copy-done.4
  128.7 0.6 copy-done.5
  129.3 4.4 %shard_map.57.turned = f32[4,512,128]{2,1,0:T(8,128)} custom-call(s32[1]{0:T(128)} %bitcast.late, f32[64,16,512]{2,1,0:T(8,128)} %middle.3, f32[64,16,512]{2,1,0:T(8,128)} %middle.3, f32[32,8,512]{2,1,0:T(8,128)} %collective-permute-done.1.mirror, f32[32,512]{1,0:T(8,128)} %copy-done.5, f32[16,512]{1,0:T(8,128)} %copy-done.4, f32[8,512]{1,0:T(8,128)} %copy-done.6, ...), custom_call_target="tpu_custom_call" | custom-call | flops 1000000000 | bytes 1048576 | tf_op jit(solution)/shard_map/pallas_call | solution.py:223
  133.8 0.0 collective-permute-done.9.mirror_up
  133.8 0.0 all-to-all-done.1
  133.8 0.0 copy-start.3
  133.8 1.0 copy-done.3
  134.7 8.0 %shard_map.58 = f32[2048,128]{1,0:T(8,128)} custom-call(s32[1]{0:T(128)} %bitcast.late, f32[64,16,512]{2,1,0:T(8,128)} %middle.3, f32[64,16,512]{2,1,0:T(8,128)} %middle.3, f32[2048,128]{1,0:T(8,128)} %bitcast.17, f32[4,512,128]{2,1,0:T(8,128)} %shard_map.57.turned, f32[32,8,512]{2,1,0:T(8,128)} %collective-permute-done.1.mirror, ...), custom_call_target="tpu_custom_call" | custom-call | flops 1000000000 | bytes 1048576 | tf_op jit(solution)/shard_map/pallas_call | solution.py:223
  142.8 0.0 copy-start
  142.8 34.4 %all_to_all.21 = f32[32,64,128]{2,1,0:T(8,128)S(1)} all-to-all(f32[32,64,128]{2,1,0:T(8,128)} %bitcast.18), channel_id=1, replica_groups=mesh['row'=8,'col'=32] {'col'}, dimensions={0} | all-to-all | bytes 2097152 | tf_op jit(solution)/shard_map/all_to_all | solution.py:245
  177.2 0.0 copy-done
  177.2 0.0 copy-start.1
  177.2 1.0 shard_map.59
  178.2 14.4 %all_to_all.22.data = f32[8,128,128]{2,1,0:T(8,128)S(1)} all-to-all(f32[8,128,128]{2,1,0:T(8,128)S(1)} %bitcast.16), channel_id=1, replica_groups=mesh['row'=8,'col'=32] {'row'}, dimensions={0} | all-to-all | bytes 1048576 | tf_op jit(solution)/shard_map/all_to_all | solution.py:245
  192.6 0.0 copy-done.1
  192.6 1.3 shard_map.60
  (8 shorter events, 0.1 us)
Async XLA Ops:
  17.5 16.3 %copy-start.2 = (f32[64,16,512]{2,1,0:T(8,128)S(1)}, f32[64,16,512]{2,1,0:T(8,128)}, u32[]{:S(2)}) copy-start(f32[64,16,512]{2,1,0:T(8,128)} %middle.3) | copy-start | bytes 6291460
  20.7 113.1 %all-to-all-start.1 = ((f32[32,64,128]{2,1,0:T(8,128)}), f32[32,64,128]{2,1,0:T(8,128)S(1)}, u32[]{:S(2)}, u32[]{:S(2)}) async-start(f32[32,64,128]{2,1,0:T(8,128)} %bitcast.19), calls=%async_computation.1 | async-start | bytes 2097152 | tf_op jit(solution)/shard_map/all_to_all | solution.py:245
  33.9 23.0 %collective-permute-start.8 = (f32[32,8,512]{2,1,0:T(8,128)S(1)}, f32[32,8,512]{2,1,0:T(8,128)}, u32[]{:S(2)}, u32[]{:S(2)}) collective-permute-start(f32[32,8,512]{2,1,0:T(8,128)S(1)} %get-tuple-element.5), channel_id=1, source_target_pairs={{0,226},{1,227},{2,224},{3,225},{4,230},{5,231},{6,228},{7,229},{8... | collective-permute-start | bytes 1572872 | tf_op jit(solution)/shard_map/ppermute | solution.py:275
  36.8 58.8 %collective-permute-start = (f32[32,8,512]{2,1,0:T(8,128)S(1)}, f32[32,8,512]{2,1,0:T(8,128)}, u32[]{:S(2)}, u32[]{:S(2)}) collective-permute-start(f32[32,8,512]{2,1,0:T(8,128)S(1)} %get-tuple-element.6), channel_id=1, source_target_pairs={{0,29},{1,28},{2,31},{3,30},{4,25},{5,24},{6,27},{7,26},{8,21},{9,... | collective-permute-start | bytes 1572872 | tf_op jit(solution)/shard_map/ppermute | solution.py:275
  56.9 76.9 %collective-permute-start.9 = (f32[32,8,512]{2,1,0:T(8,128)}, f32[32,8,512]{2,1,0:T(8,128)}, u32[]{:S(2)}, u32[]{:S(2)}) collective-permute-start(f32[32,8,512]{2,1,0:T(8,128)} %collective-permute-done.8), channel_id=1, source_target_pairs={{0,29},{1,28},{2,31},{3,30},{4,25},{5,24},{6,27},{7,26},{8,21},{9,... | collective-permute-start | bytes 1572872 | tf_op jit(solution)/shard_map/ppermute | solution.py:275
  95.6 33.1 %collective-permute-start.1 = (f32[32,8,512]{2,1,0:T(8,128)}, f32[32,8,512]{2,1,0:T(8,128)}, u32[]{:S(2)}, u32[]{:S(2)}) collective-permute-start(f32[32,8,512]{2,1,0:T(8,128)} %collective-permute-done), channel_id=1, source_target_pairs={{0,226},{1,227},{2,224},{3,225},{4,230},{5,231},{6,228},{7,229},{8... | collective-permute-start | bytes 1572872 | tf_op jit(solution)/shard_map/ppermute | solution.py:275
  98.3 13.1 %collective-permute-start.3 = (f32[16,512]{1,0:T(8,128)S(1)}, f32[16,512]{1,0:T(8,128)S(1)}, u32[]{:S(2)}, u32[]{:S(2)}) collective-permute-start(f32[16,512]{1,0:T(8,128)S(1)} %slice_bitcast_fusion), channel_id=1, source_target_pairs={{0,31},{1,30},{2,29},{3,28},{4,27},{5,26},{6,25},{7,24},{8,23},{9,... | collective-permute-start | bytes 98312 | tf_op jit(solution)/shard_map/ppermute | solution.py:254
  98.4 12.4 %collective-permute-start.4 = (f32[8,512]{1,0:T(8,128)S(1)}, f32[8,512]{1,0:T(8,128)S(1)}, u32[]{:S(2)}, u32[]{:S(2)}) collective-permute-start(f32[8,512]{1,0:T(8,128)S(1)} %broadcast_in_dim.16), channel_id=1, source_target_pairs={{0,0},{1,31},{2,30},{3,29},{4,28},{5,27},{6,26},{7,25},{8,24},{9,2... | collective-permute-start | bytes 49160 | tf_op jit(solution)/shard_map/ppermute | solution.py:254
  110.7 18.0 %copy-start.6 = (f32[8,512]{1,0:T(8,128)}, f32[8,512]{1,0:T(8,128)S(1)}, u32[]{:S(2)}) copy-start(f32[8,512]{1,0:T(8,128)S(1)} %collective-permute-done.4.start_edge) | copy-start | bytes 49156
  111.5 17.3 %copy-start.4 = (f32[16,512]{1,0:T(8,128)}, f32[16,512]{1,0:T(8,128)S(1)}, u32[]{:S(2)}) copy-start(f32[16,512]{1,0:T(8,128)S(1)} %collective-permute-done.3.start) | copy-start | bytes 98308
  111.5 3.8 %collective-permute-start.5 = (f32[40,512]{1,0:T(8,128)S(1)}, f32[40,512]{1,0:T(8,128)S(1)}, u32[]{:S(2)}, u32[]{:S(2)}) collective-permute-start(f32[40,512]{1,0:T(8,128)S(1)} %maximum_select_fusion), channel_id=1, source_target_pairs={{0,128},{1,129},{2,130},{3,131},{4,132},{5,133},{6,134},{7,135},{8... | collective-permute-start | bytes 245768 | tf_op jit(solution)/shard_map/ppermute | solution.py:261
  115.3 3.1 %collective-permute-start.6 = (f32[40,512]{1,0:T(8,128)S(1)}, f32[40,512]{1,0:T(8,128)S(1)}, u32[]{:S(2)}, u32[]{:S(2)}) collective-permute-start(f32[40,512]{1,0:T(8,128)S(1)} %add.13), channel_id=1, source_target_pairs={{0,64},{128,192},{1,65},{129,193},{2,66},{130,194},{3,67},{131,195... | collective-permute-start | bytes 245768 | tf_op jit(solution)/shard_map/ppermute | solution.py:261
  118.4 2.8 %collective-permute-start.7 = (f32[40,512]{1,0:T(8,128)S(1)}, f32[40,512]{1,0:T(8,128)S(1)}, u32[]{:S(2)}, u32[]{:S(2)}) collective-permute-start(f32[40,512]{1,0:T(8,128)S(1)} %add.14), channel_id=1, source_target_pairs={{0,32},{64,96},{128,160},{192,224},{1,33},{65,97},{129,161},{193,2... | collective-permute-start | bytes 245768 | tf_op jit(solution)/shard_map/ppermute | solution.py:261
  119.8 8.9 %collective-permute-start.2 = (f32[32,512]{1,0:T(8,128)S(1)}, f32[32,512]{1,0:T(8,128)S(1)}, u32[]{:S(2)}, u32[]{:S(2)}) collective-permute-start(f32[32,512]{1,0:T(8,128)S(1)} %bitcast.21), channel_id=1, source_target_pairs={{0,224},{1,255},{2,254},{3,253},{4,252},{5,251},{6,250},{7,249},{8... | collective-permute-start | bytes 196616 | tf_op jit(solution)/shard_map/ppermute | solution.py:254
  128.7 0.6 copy-start.5
  133.8 1.0 copy-start.3
  142.8 34.4 %copy-start = (bf16[2,2,256,256]{3,2,1,0:T(8,128)(2,1)S(1)}, bf16[2,2,256,256]{3,2,1,0:T(8,128)(2,1)}, u32[]{:S(2)}) copy-start(bf16[2,2,256,256]{3,2,1,0:T(8,128)(2,1)} %constant.20.clone.backward) | copy-start | bytes 1572868
  177.2 15.5 %copy-start.1 = (bf16[2,512,256]{2,1,0:T(8,128)(2,1)S(1)}, bf16[2,512,256]{2,1,0:T(8,128)(2,1)}, u32[]{:S(2)}) copy-start(bf16[2,512,256]{2,1,0:T(8,128)(2,1)} %constant.18.clone.table) | copy-start | bytes 1572868

commit v5 on v4

--- a/solution.py
+++ b/solution.py
@@ -191,11 +191,11 @@
     turn_green(0, late, green, middle, mirror, None, mirror_edge, start, start_edge, zero, out)
 
 
-def x_both(
-    late, green, middle, data, turned, mirror, mirror_up, start, zero, forward, backward, out, turned_up
-):
-    turn_green(1, late, green, middle, mirror, mirror_up, None, start, None, zero, turned_up)
-
+def turn_second(late, green, middle, mirror, mirror_up, start, zero, out):
+    turn_green(1, late, green, middle, mirror, mirror_up, None, start, None, zero, out)
+
+
+def x_both(data, turned, turned_up, forward, backward, out):
     def step(own, at, k):
         k = at + 2 * k
         cols = [
@@ -226,7 +226,7 @@
         grid=(1,) if blocks else (),
         in_specs=[smem] * scalars + [*blocks] + [vmem] * (len(args) - scalars - len(blocks)),
         out_specs=vmem,
-        scratch_shapes=[pltpu.VMEM(s, jnp.float32) for s in scratch],
+        scratch_shapes=scratch,
         compiler_params=pltpu.CompilerParams(vmem_limit_bytes=grant * 1024 * 1024),
         cost_estimate=pl.CostEstimate(
             flops=10**9, bytes_accessed=4 * int(np.prod(shape)), transcendentals=0
@@ -264,13 +264,15 @@
 
 def on_device(charge, green):
     z_table, forward, backward = (jnp.asarray(t) for t in tables())
+    along_z = call(z_forward, (8, LANES, LANES), 60, charge.reshape(256, N), z_table)
+    later, along_z = lax.optimization_barrier((green, along_z))
     moves = {
         "mirror": ("col", [(j, j ^ 29) for j in range(32)]),
         "across": (("row", "col"), [(i, i ^ 226) for i in range(256)]),
     }
     mirrors = []
     for k, order in enumerate((("mirror", "across"), ("across", "mirror"))):
-        half = green[SLOTS:, 8 * (1 - k) : 8 * (2 - k)]
+        half = (green, later)[k][SLOTS:, 8 * (1 - k) : 8 * (2 - k)]
         for name in order:
             half = lax.ppermute(half, *moves[name])
         mirrors.append(half)
@@ -284,18 +286,18 @@
         turn_first, (4, M, LANES), 60, late, green, green, mirrors[0], mirror_edge, start, start_edge,
         zero, scalars=1, blocks=green_blocks(0),
     )
-    along_z = call(z_forward, (8, LANES, LANES), 60, charge.reshape(256, N), z_table)
+    turned_up = call(
+        turn_second, (4, M, LANES), 60, late, green, green, *mirrors, start, zero,
+        scalars=1, blocks=green_blocks(1),
+    )
     by_rows = exchange(along_z, "row").reshape(1024, LANES)
-    along_y = call(y_forward, (32, 8, 8, LANES), 60, by_rows, forward, scratch=[(2 * M, LANES)])
+    along_y = call(y_forward, (32, 8, 8, LANES), 16, by_rows, forward, scratch=[pltpu.VMEM((2 * M, LANES), jnp.float32)])
     by_cols = exchange(along_y.reshape(32, HALF, LANES), "col").reshape(2048, LANES)
-    back_x = call(
-        x_both, (2048, LANES), 60, late, green, green, by_cols, turned, *mirrors, start, zero,
-        forward, backward, scalars=1, blocks=green_blocks(1), scratch=[(4, M, LANES)],
-    )
+    back_x = call(x_both, (2048, LANES), 24, by_cols, turned, turned_up, forward, backward)
     by_cells = exchange(back_x.reshape(32, HALF, LANES), "col")
     back_y = call(
         y_backward, (1024, LANES), 16, by_cells.reshape(32, 8, 8, LANES), backward,
-        scratch=[(2 * M, LANES)],
+        scratch=[pltpu.VMEM((2 * M, LANES), jnp.float32)],
     )
     by_parts = exchange(back_y.reshape(8, LANES, LANES), "row")
     back_z = call(z_backward, (256, N), 16, by_parts, z_table)

time: 196 us -> 197 us (level)
  local copies, waits for them, and re-layouts: 1.72 us -> 7.52 us
  starting transfers between devices: 38.2 us -> 34.7 us
  blocking collectives: 63.7 us -> 66.8 us
  waiting for transfers between devices: 68.9 us -> 66.5 us
    ppermute x4, starting transfers between devices: 14.5 us -> 8.96 us  [on_device(): half = lax.ppermute(half, *moves[name])]
    ppermute x3, waiting for transfers between devices: 13.6 us -> 10.3 us  [reflect(): return lax.ppermute(value, ('row', 'col'), pairs)]
    all_to_all x3, blocking collectives: 63.7 us -> 66.8 us  [exchange(): return lax.all_to_all(value, axis, split_axis=0, concat_axis=0, tiled=True)]
    ppermute x4, waiting for transfers between devices: 50 us -> 53.1 us  [on_device(): half = lax.ppermute(half, *moves[name])]
    ppermute x3, waiting for transfers between devices: 5.32 us -> 3.19 us  [spread(): value = value + lax.ppermute(value, 'row', pairs)]
    slice x1 -> x2, local copies, waits for them, and re-layouts: 0.08 us -> 2.15 us  [on_device(): half = (green, later)[k][SLOTS:, 8 * (1 - k):8 * (2 - k)]]
    pallas_call x6 -> x7, Pallas kernels: 20.6 us -> 18.7 us  [call(): pl.pallas_call(body, out_shape=jax.ShapeDtypeStruct(shape, jnp.float32),...]
  transfers between devices with their start and end apart: 11 -> 11, of which waited for: 8 -> 7; matrix products, arithmetic and copies ran while one was open for 0% -> 3% of each run, Pallas kernels for 2% -> 5%
where the time goes in v5:
time: 197 us; the launch traced here: 195 us
  blocking collectives  66.8 us (34%)
  waiting for transfers between devices  66.5 us (34%)
  starting transfers between devices  34.7 us (18%)
  Pallas kernels  18.7 us (9%)
  local copies, waits for them, and re-layouts  7.52 us (4%)
    all_to_all x3, blocking collectives, exchange(): return lax.all_to_all(value, axis, split_axis=0, concat_axis=0, tiled=True)  66.8 us
    ppermute x4, waiting for transfers between devices, on_device(): half = lax.ppermute(half, *moves[name])  53.1 us
    pallas_call x7, Pallas kernels, call(): pl.pallas_call(body, out_shape=jax.ShapeDtypeStruct(shape, jnp.float32),...  18.7 us
    all_to_all x1, starting transfers between devices, exchange(): return lax.all_to_all(value, axis, split_axis=0, concat_axis=0, tiled=True)  12.8 us
    ppermute x3, waiting for transfers between devices, reflect(): return lax.ppermute(value, ('row', 'col'), pairs)  10.3 us
    ppermute x4, starting transfers between devices, on_device(): half = lax.ppermute(half, *moves[name])  8.96 us
    ppermute x3, starting transfers between devices, reflect(): return lax.ppermute(value, ('row', 'col'), pairs)  7.07 us
    ppermute x3, starting transfers between devices, spread(): value = value + lax.ppermute(value, 'row', pairs)  5.87 us
  transfers between devices with their start and end apart: 11, of which 7 were waited for; matrix products, arithmetic and copies ran while one was open for 3% of the time, Pallas kernels for 5%

profile of v5, /device:TPU:1, one launch (start us, length us, event | category | flops | bytes accessed | tf_op | source)
XLA Modules:
  0.0 195.1 jit_solution(3410954303729645315)
XLA Ops:
  0.0 0.0 copy-start.3
  0.0 2.6 %shard_map.55 = f32[8,128,128]{2,1,0:T(8,128)} custom-call(f32[256,256]{1,0:T(8,128)} %bitcast.22, bf16[2,512,256]{2,1,0:T(8,128)(2,1)} %constant.18.clone.table), custom_call_target="tpu_custom_call" | custom-call | flops 1000000000 | bytes 524288 | tf_op jit(solution)/shard_map/pallas_call | solution.py:223
  2.6 15.1 %all_to_all.20 = f32[8,128,128]{2,1,0:T(8,128)S(1)} all-to-all(f32[8,128,128]{2,1,0:T(8,128)} %shard_map.55), channel_id=1, replica_groups=mesh['row'=8,'col'=32] {'row'}, dimensions={0} | all-to-all | bytes 1048576 | tf_op jit(solution)/shard_map/all_to_all | solution.py:245
  17.7 0.0 copy-done.3
  17.7 1.9 shard_map.56
  19.6 12.8 %all-to-all-start.1 = ((f32[32,64,128]{2,1,0:T(8,128)}), f32[32,64,128]{2,1,0:T(8,128)S(1)}, u32[]{:S(2)}, u32[]{:S(2)}) async-start(f32[32,64,128]{2,1,0:T(8,128)} %bitcast.2), calls=%async_computation.1 | async-start | bytes 2097152 | tf_op jit(solution)/shard_map/all_to_all | solution.py:245
  32.4 1.1 slice.16
  33.5 3.0 %collective-permute-start = (f32[32,8,512]{2,1,0:T(8,128)S(1)}, f32[32,8,512]{2,1,0:T(8,128)}, u32[]{:S(2)}, u32[]{:S(2)}) collective-permute-start(f32[32,8,512]{2,1,0:T(8,128)S(1)} %slice.16), channel_id=1, source_target_pairs={{0,29},{1,28},{2,31},{3,30},{4,25},{5,24},{6,27},{7,26},{8,21},{9,... | collective-permute-start | bytes 1572872 | tf_op jit(solution)/shard_map/ppermute | solution.py:277
  36.5 1.1 slice.20
  37.5 2.8 %collective-permute-start.8 = (f32[32,8,512]{2,1,0:T(8,128)S(1)}, f32[32,8,512]{2,1,0:T(8,128)}, u32[]{:S(2)}, u32[]{:S(2)}) collective-permute-start(f32[32,8,512]{2,1,0:T(8,128)S(1)} %slice.20), channel_id=1, source_target_pairs={{0,226},{1,227},{2,224},{3,225},{4,230},{5,231},{6,228},{7,229},{8... | collective-permute-start | bytes 1572872 | tf_op jit(solution)/shard_map/ppermute | solution.py:277
  40.3 53.1 %collective-permute-done = f32[32,8,512]{2,1,0:T(8,128)} collective-permute-done((f32[32,8,512]{2,1,0:T(8,128)S(1)}, f32[32,8,512]{2,1,0:T(8,128)}, u32[]{:S(2)}, u32[]{:S(2)}) %collective-permute-start) | collective-permute-done | bytes 524320 | tf_op jit(solution)/shard_map/ppermute | solution.py:277
  93.4 2.7 %collective-permute-start.1 = (f32[32,8,512]{2,1,0:T(8,128)}, f32[32,8,512]{2,1,0:T(8,128)S(1)}, u32[]{:S(2)}, u32[]{:S(2)}) collective-permute-start(f32[32,8,512]{2,1,0:T(8,128)} %collective-permute-done), channel_id=1, source_target_pairs={{0,226},{1,227},{2,224},{3,225},{4,230},{5,231},{6,228},{7,229},{8... | collective-permute-start | bytes 1572872 | tf_op jit(solution)/shard_map/ppermute | solution.py:277
  96.1 0.0 collective-permute-done.8
  96.1 0.5 collective-permute-start.9
  96.6 0.8 slice_bitcast_fusion
  97.3 2.2 %collective-permute-start.3 = (f32[16,512]{1,0:T(8,128)S(1)}, f32[16,512]{1,0:T(8,128)S(1)}, u32[]{:S(2)}, u32[]{:S(2)}) collective-permute-start(f32[16,512]{1,0:T(8,128)S(1)} %slice_bitcast_fusion), channel_id=1, source_target_pairs={{0,31},{1,30},{2,29},{3,28},{4,27},{5,26},{6,25},{7,24},{8,23},{9,... | collective-permute-start | bytes 98312 | tf_op jit(solution)/shard_map/ppermute | solution.py:254
  99.5 0.7 slice.19
  100.3 4.8 %collective-permute-start.4 = (f32[8,512]{1,0:T(8,128)S(1)}, f32[8,512]{1,0:T(8,128)S(1)}, u32[]{:S(2)}, u32[]{:S(2)}) collective-permute-start(f32[8,512]{1,0:T(8,128)S(1)} %broadcast_in_dim.16), channel_id=1, source_target_pairs={{0,0},{1,31},{2,30},{3,29},{4,28},{5,27},{6,26},{7,25},{8,24},{9,2... | collective-permute-start | bytes 49160 | tf_op jit(solution)/shard_map/ppermute | solution.py:254
  105.0 7.7 %collective-permute-done.4.start_edge = f32[8,512]{1,0:T(8,128)S(1)} collective-permute-done((f32[8,512]{1,0:T(8,128)S(1)}, f32[8,512]{1,0:T(8,128)S(1)}, u32[]{:S(2)}, u32[]{:S(2)}) %collective-permute-start.4) | collective-permute-done | bytes 16416 | tf_op jit(solution)/shard_map/ppermute | solution.py:254
  112.8 0.0 copy-start.9
  112.8 0.4 collective-permute-done.3.start
  113.2 0.0 copy-start.7
  113.2 3.3 %collective-permute-start.5 = (f32[40,512]{1,0:T(8,128)S(1)}, f32[40,512]{1,0:T(8,128)S(1)}, u32[]{:S(2)}, u32[]{:S(2)}) collective-permute-start(f32[40,512]{1,0:T(8,128)S(1)} %maximum_select_fusion), channel_id=1, source_target_pairs={{0,128},{1,129},{2,130},{3,131},{4,132},{5,133},{6,134},{7,135},{8... | collective-permute-start | bytes 245768 | tf_op jit(solution)/shard_map/ppermute | solution.py:261
  116.5 1.5 collective-permute-done.5
  118.0 1.3 collective-permute-start.6
  119.3 1.5 collective-permute-done.6
  120.7 1.3 collective-permute-start.7
  122.0 1.1 slice.17
  123.1 0.1 collective-permute-start.2
  123.2 0.3 collective-permute-done.7
  123.5 0.6 add.15.zero
  124.1 0.0 collective-permute-done.1.mirror
  124.2 0.0 copy-start.5
  124.2 0.0 collective-permute-done.9.mirror_up
  124.2 0.0 copy-start.6
  124.2 0.0 copy-done.7
  124.2 0.8 copy-done.5
  124.9 0.2 copy-done.6
  125.1 4.5 %shard_map.58.turned_up = f32[4,512,128]{2,1,0:T(8,128)} custom-call(s32[1]{0:T(128)} %bitcast.4.late, f32[64,16,512]{2,1,0:T(8,128)} %middle.3, f32[64,16,512]{2,1,0:T(8,128)} %middle.3, f32[32,8,512]{2,1,0:T(8,128)} %copy-done.5, f32[32,8,512]{2,1,0:T(8,128)} %copy-done.6, f32[16,512]{1,0:T(8,128)} %copy-done.7, f32[40,512]{1,0:T(8,128)} %add.15.zero), custom_call_target="tpu_custom_call" | custom-call | flops 1000000000 | bytes 1048576 | tf_op jit(solution)/shard_map/pallas_call | solution.py:223
  129.6 0.0 copy-done.9
  129.6 0.0 copy-start
  129.6 0.0 copy-start.2
  129.6 2.1 %collective-permute-done.2.mirror_edge = f32[32,512]{1,0:T(8,128)S(1)} collective-permute-done((f32[32,512]{1,0:T(8,128)S(1)}, f32[32,512]{1,0:T(8,128)S(1)}, u32[]{:S(2)}, u32[]{:S(2)}) %collective-permute-start.2) | collective-permute-done | bytes 65568 | tf_op jit(solution)/shard_map/ppermute | solution.py:254
  131.8 0.0 copy-start.8
  131.8 0.6 copy-done.8
  132.4 4.4 %shard_map.57.turned = f32[4,512,128]{2,1,0:T(8,128)} custom-call(s32[1]{0:T(128)} %bitcast.4.late, f32[64,16,512]{2,1,0:T(8,128)} %middle.3, f32[64,16,512]{2,1,0:T(8,128)} %middle.3, f32[32,8,512]{2,1,0:T(8,128)} %copy-done.5, f32[32,512]{1,0:T(8,128)} %copy-done.8, f32[16,512]{1,0:T(8,128)} %copy-done.7, f32[8,512]{1,0:T(8,128)} %copy-done.9, ...), custom_call_target="tpu_custom_call" | custom-call | flops 1000000000 | bytes 1048576 | tf_op jit(solution)/shard_map/pallas_call | solution.py:223
  136.8 0.0 all-to-all-done.1
  136.8 0.0 copy-done
  136.8 0.0 copy-done.2
  136.8 0.0 copy-start.1
  136.8 1.2 copy-done.1
  138.0 2.9 %shard_map.59 = f32[2048,128]{1,0:T(8,128)S(1)} custom-call(f32[2048,128]{1,0:T(8,128)S(1)} %bitcast.15, f32[4,512,128]{2,1,0:T(8,128)S(1)} %copy-done.1, f32[4,512,128]{2,1,0:T(8,128)S(1)} %copy-done, bf16[2,2,256,256]{3,2,1,0:T(8,128)(2,1)S(1)} %copy-done.3, bf16[2,2,256,256]{3,2,1,0:T(8,128)(2,1)S(1)} %copy-done.2), custom_call_target="tpu_custom_call" | custom-call | flops 1000000000 | bytes 1048576 | tf_op jit(solution)/shard_map/pallas_call | solution.py:223
  140.9 36.9 %all_to_all.21 = f32[32,64,128]{2,1,0:T(8,128)S(1)} all-to-all(f32[32,64,128]{2,1,0:T(8,128)S(1)} %bitcast.16), channel_id=1, replica_groups=mesh['row'=8,'col'=32] {'col'}, dimensions={0} | all-to-all | bytes 2097152 | tf_op jit(solution)/shard_map/all_to_all | solution.py:245
  177.9 0.0 copy-start.4
  177.9 1.0 shard_map.60
  178.9 14.8 %all_to_all.22.data = f32[8,128,128]{2,1,0:T(8,128)S(1)} all-to-all(f32[8,128,128]{2,1,0:T(8,128)S(1)} %bitcast.18), channel_id=1, replica_groups=mesh['row'=8,'col'=32] {'row'}, dimensions={0} | all-to-all | bytes 1048576 | tf_op jit(solution)/shard_map/all_to_all | solution.py:245
  193.7 0.0 copy-done.4
  193.8 1.3 shard_map.61
  (5 shorter events, 0.0 us)
Async XLA Ops:
  0.0 17.7 %copy-start.3 = (bf16[2,2,256,256]{3,2,1,0:T(8,128)(2,1)S(1)}, bf16[2,2,256,256]{3,2,1,0:T(8,128)(2,1)}, u32[]{:S(2)}) copy-start(bf16[2,2,256,256]{3,2,1,0:T(8,128)(2,1)} %constant.19.clone.table.forward) | copy-start | bytes 1572868
  19.6 117.2 %all-to-all-start.1 = ((f32[32,64,128]{2,1,0:T(8,128)}), f32[32,64,128]{2,1,0:T(8,128)S(1)}, u32[]{:S(2)}, u32[]{:S(2)}) async-start(f32[32,64,128]{2,1,0:T(8,128)} %bitcast.2), calls=%async_computation.1 | async-start | bytes 2097152 | tf_op jit(solution)/shard_map/all_to_all | solution.py:245
  33.5 59.9 %collective-permute-start = (f32[32,8,512]{2,1,0:T(8,128)S(1)}, f32[32,8,512]{2,1,0:T(8,128)}, u32[]{:S(2)}, u32[]{:S(2)}) collective-permute-start(f32[32,8,512]{2,1,0:T(8,128)S(1)} %slice.16), channel_id=1, source_target_pairs={{0,29},{1,28},{2,31},{3,30},{4,25},{5,24},{6,27},{7,26},{8,21},{9,... | collective-permute-start | bytes 1572872 | tf_op jit(solution)/shard_map/ppermute | solution.py:277
  37.5 58.6 %collective-permute-start.8 = (f32[32,8,512]{2,1,0:T(8,128)S(1)}, f32[32,8,512]{2,1,0:T(8,128)}, u32[]{:S(2)}, u32[]{:S(2)}) collective-permute-start(f32[32,8,512]{2,1,0:T(8,128)S(1)} %slice.20), channel_id=1, source_target_pairs={{0,226},{1,227},{2,224},{3,225},{4,230},{5,231},{6,228},{7,229},{8... | collective-permute-start | bytes 1572872 | tf_op jit(solution)/shard_map/ppermute | solution.py:277
  93.4 30.8 %collective-permute-start.1 = (f32[32,8,512]{2,1,0:T(8,128)}, f32[32,8,512]{2,1,0:T(8,128)S(1)}, u32[]{:S(2)}, u32[]{:S(2)}) collective-permute-start(f32[32,8,512]{2,1,0:T(8,128)} %collective-permute-done), channel_id=1, source_target_pairs={{0,226},{1,227},{2,224},{3,225},{4,230},{5,231},{6,228},{7,229},{8... | collective-permute-start | bytes 1572872 | tf_op jit(solution)/shard_map/ppermute | solution.py:277
  96.1 28.1 %collective-permute-start.9 = (f32[32,8,512]{2,1,0:T(8,128)}, f32[32,8,512]{2,1,0:T(8,128)S(1)}, u32[]{:S(2)}, u32[]{:S(2)}) collective-permute-start(f32[32,8,512]{2,1,0:T(8,128)} %collective-permute-done.8), channel_id=1, source_target_pairs={{0,29},{1,28},{2,31},{3,30},{4,25},{5,24},{6,27},{7,26},{8,21},{9,... | collective-permute-start | bytes 1572872 | tf_op jit(solution)/shard_map/ppermute | solution.py:277
  97.3 15.8 %collective-permute-start.3 = (f32[16,512]{1,0:T(8,128)S(1)}, f32[16,512]{1,0:T(8,128)S(1)}, u32[]{:S(2)}, u32[]{:S(2)}) collective-permute-start(f32[16,512]{1,0:T(8,128)S(1)} %slice_bitcast_fusion), channel_id=1, source_target_pairs={{0,31},{1,30},{2,29},{3,28},{4,27},{5,26},{6,25},{7,24},{8,23},{9,... | collective-permute-start | bytes 98312 | tf_op jit(solution)/shard_map/ppermute | solution.py:254
  100.3 12.5 %collective-permute-start.4 = (f32[8,512]{1,0:T(8,128)S(1)}, f32[8,512]{1,0:T(8,128)S(1)}, u32[]{:S(2)}, u32[]{:S(2)}) collective-permute-start(f32[8,512]{1,0:T(8,128)S(1)} %broadcast_in_dim.16), channel_id=1, source_target_pairs={{0,0},{1,31},{2,30},{3,29},{4,28},{5,27},{6,26},{7,25},{8,24},{9,2... | collective-permute-start | bytes 49160 | tf_op jit(solution)/shard_map/ppermute | solution.py:254
  112.8 16.9 %copy-start.9 = (f32[8,512]{1,0:T(8,128)}, f32[8,512]{1,0:T(8,128)S(1)}, u32[]{:S(2)}) copy-start(f32[8,512]{1,0:T(8,128)S(1)} %collective-permute-done.4.start_edge) | copy-start | bytes 49156
  113.2 11.0 %copy-start.7 = (f32[16,512]{1,0:T(8,128)}, f32[16,512]{1,0:T(8,128)S(1)}, u32[]{:S(2)}) copy-start(f32[16,512]{1,0:T(8,128)S(1)} %collective-permute-done.3.start) | copy-start | bytes 98308
  113.2 4.8 %collective-permute-start.5 = (f32[40,512]{1,0:T(8,128)S(1)}, f32[40,512]{1,0:T(8,128)S(1)}, u32[]{:S(2)}, u32[]{:S(2)}) collective-permute-start(f32[40,512]{1,0:T(8,128)S(1)} %maximum_select_fusion), channel_id=1, source_target_pairs={{0,128},{1,129},{2,130},{3,131},{4,132},{5,133},{6,134},{7,135},{8... | collective-permute-start | bytes 245768 | tf_op jit(solution)/shard_map/ppermute | solution.py:261
  118.0 2.8 %collective-permute-start.6 = (f32[40,512]{1,0:T(8,128)S(1)}, f32[40,512]{1,0:T(8,128)S(1)}, u32[]{:S(2)}, u32[]{:S(2)}) collective-permute-start(f32[40,512]{1,0:T(8,128)S(1)} %add.13), channel_id=1, source_target_pairs={{0,64},{128,192},{1,65},{129,193},{2,66},{130,194},{3,67},{131,195... | collective-permute-start | bytes 245768 | tf_op jit(solution)/shard_map/ppermute | solution.py:261
  120.7 2.8 %collective-permute-start.7 = (f32[40,512]{1,0:T(8,128)S(1)}, f32[40,512]{1,0:T(8,128)S(1)}, u32[]{:S(2)}, u32[]{:S(2)}) collective-permute-start(f32[40,512]{1,0:T(8,128)S(1)} %add.14), channel_id=1, source_target_pairs={{0,32},{64,96},{128,160},{192,224},{1,33},{65,97},{129,161},{193,2... | collective-permute-start | bytes 245768 | tf_op jit(solution)/shard_map/ppermute | solution.py:261
  123.1 8.6 %collective-permute-start.2 = (f32[32,512]{1,0:T(8,128)S(1)}, f32[32,512]{1,0:T(8,128)S(1)}, u32[]{:S(2)}, u32[]{:S(2)}) collective-permute-start(f32[32,512]{1,0:T(8,128)S(1)} %bitcast.20), channel_id=1, source_target_pairs={{0,224},{1,255},{2,254},{3,253},{4,252},{5,251},{6,250},{7,249},{8... | collective-permute-start | bytes 196616 | tf_op jit(solution)/shard_map/ppermute | solution.py:254
  124.2 0.8 copy-start.5
  124.2 1.0 copy-start.6
  129.6 7.2 %copy-start = (f32[4,512,128]{2,1,0:T(8,128)S(1)}, f32[4,512,128]{2,1,0:T(8,128)}, u32[]{:S(2)}) copy-start(f32[4,512,128]{2,1,0:T(8,128)} %shard_map.58.turned_up) | copy-start | bytes 3145732
  129.6 7.2 %copy-start.2 = (bf16[2,2,256,256]{3,2,1,0:T(8,128)(2,1)S(1)}, bf16[2,2,256,256]{3,2,1,0:T(8,128)(2,1)}, u32[]{:S(2)}) copy-start(bf16[2,2,256,256]{3,2,1,0:T(8,128)(2,1)} %constant.20.clone.backward) | copy-start | bytes 1572868
  131.8 0.6 copy-start.8
  136.8 1.2 copy-start.1
  177.9 15.9 %copy-start.4 = (bf16[2,512,256]{2,1,0:T(8,128)(2,1)S(1)}, bf16[2,512,256]{2,1,0:T(8,128)(2,1)}, u32[]{:S(2)}) copy-start(bf16[2,512,256]{2,1,0:T(8,128)(2,1)} %constant.18.clone.table) | copy-start | bytes 1572868

commit v6 on v5

--- a/solution.py
+++ b/solution.py
@@ -151,7 +151,7 @@
     out[...] = total * (1.0 / M**3)
 
 
-def turn_green(up, late, green, middle, mirror, mirror_up, mirror_edge, start, start_edge, zero, out):
+def turn_green(lows, base, late, green, middle, low, high, mirror_edge, start, start_edge, zero, out):
     late, own_mirror = late[0] > 0, late[0] > 1
     slot = lax.broadcasted_iota(jnp.int32, (SLOTS, M), 0)
     sign = jnp.where(slot % 2 == 1, 1.0, -1.0)
@@ -167,43 +167,53 @@
     def rows(array, at):
         return jnp.broadcast_to(array[at : at + 1, :], (SLOTS, M))
 
-    for k in range(4):
+    parts = []
+    for k, b_low in enumerate(lows):
         owns, others = [], []
-        for b in (8 * up + 2 * k, 8 * up + 2 * k + 1):
-            at = b - 8 * up
+        for b in (2 * b_low, 2 * b_low + 1):
+            at = b - base
             mid = jnp.broadcast_to(middle[0, at : at + 1, :], (SLOTS, M))
             own = jnp.where((slot == 0) & ~late, mid, green[:, at, :])
             owns.append((own + sign * rows(zero, b)) * share)
             if b == 0:
                 other, begin, nil = mirror_edge[...], rows(start_edge, 0), rows(zero, 32)
             else:
-                other = mirror[:, 8 - b, :] if b <= 8 else mirror_up[:, 16 - b, :]
+                other = high[:, 8 - b, :] if b <= 8 else low[:, 16 - b, :]
                 begin, nil = rows(start, 16 - b), rows(zero, 32 - b)
             other = jnp.where((slot == 0) & late, begin, other)
             others.append((other + sign * nil) * share)
         own = jnp.concatenate([owns[0], owns[0], owns[1], owns[1]], 0)
         oh, ol = halves(jnp.concatenate(others, 0))
-        oh, ol = halves(dot(turn, oh, nn) + dot(turn, ol, nn))
-        out[k] = own.T + (dot(swap, oh, nt) + dot(swap, ol, nt))
-
-
-def turn_first(late, green, middle, mirror, mirror_edge, start, start_edge, zero, out):
-    turn_green(0, late, green, middle, mirror, None, mirror_edge, start, start_edge, zero, out)
-
-
-def turn_second(late, green, middle, mirror, mirror_up, start, zero, out):
-    turn_green(1, late, green, middle, mirror, mirror_up, None, start, None, zero, out)
-
-
-def x_both(data, turned, turned_up, forward, backward, out):
-    def step(own, at, k):
-        k = at + 2 * k
+        parts.append(halves(dot(turn, oh, nn) + dot(turn, ol, nn)))
+        out[k] = own.T
+    oh, ol = (jnp.concatenate([p[i] for p in parts], 0) for i in range(2))
+    both = dot(swap, oh, nt) + dot(swap, ol, nt)
+    for k in range(len(lows)):
+        out[k] += both[:, LANES * k : LANES * (k + 1)]
+
+
+def turn_first(late, green, middle, low, start, zero, out):
+    turn_green(range(5, 8), 8, late, green, middle, low, None, None, start, None, zero, out)
+
+
+def turn_second(late, green, middle, low, high, mirror_edge, start, start_edge, zero, out):
+    turn_green(
+        range(5), 0, late, green, middle, low, high, mirror_edge, start, start_edge, zero, out
+    )
+
+
+def x_both(data, turned_up, turned, forward, backward, out):
+    def green(b_low, h):
+        own, at = (turned, b_low) if b_low < 5 else (turned_up, b_low - 5)
+        return own[at, N * h : N * (h + 1)]
+
+    for k in range(0, 8, 2):
         cols = [
             [data[pl.ds(8 * p + k + i, LANES, stride=16), :] for i in range(2)] for p in range(2)
         ]
         even, odd = both_parities(forward, cols)
         low, high = (
-            jnp.concatenate([own[k - at + i, N * h : N * (h + 1)] for i in range(2)], 1)
+            jnp.concatenate([green(k + i, h) for i in range(2)], 1)
             for h in range(2)
         )
         low, high = (even + odd) * low, (even - odd) * high
@@ -212,10 +222,6 @@
             for i in range(2):
                 field = backward_join(both[:, LANES * i : LANES * (i + 1)])
                 out[pl.ds(8 * p + k + i, LANES, stride=16), :] = field
-
-    for at, own in ((0, turned), (4, turned_up)):
-        for k in range(2):
-            step(own, at, k)
 
 
 def call(body, shape, grant, *args, scalars=0, scratch=(), blocks=()):
@@ -234,10 +240,10 @@
     )(*args)
 
 
-def green_blocks(up):
+def green_blocks(length, at):
     return [
-        pl.BlockSpec((SLOTS, 8, M), lambda i: (0, up, 0)),
-        pl.BlockSpec((1, 8, M), lambda i: (SLOTS, up, 0)),
+        pl.BlockSpec((SLOTS, length, M), lambda i: (0, at, 0)),
+        pl.BlockSpec((1, length, M), lambda i: (SLOTS, at, 0)),
     ]
 
 
@@ -272,7 +278,7 @@
     }
     mirrors = []
     for k, order in enumerate((("mirror", "across"), ("across", "mirror"))):
-        half = (green, later)[k][SLOTS:, 8 * (1 - k) : 8 * (2 - k)]
+        half = (green, later)[k][SLOTS:, 8 * k : 8 * (k + 1)]
         for name in order:
             half = lax.ppermute(half, *moves[name])
         mirrors.append(half)
@@ -282,18 +288,18 @@
     zero = spread(jnp.concatenate([green[0], start, start_edge], 0))
     row = lax.axis_index("row")
     late = ((row >= 4).astype(jnp.int32) + (row == 4).astype(jnp.int32))[None]
+    turned_up = call(
+        turn_first, (3, M, LANES), 60, late, green, green, mirrors[0], start, zero,
+        scalars=1, blocks=green_blocks(8, 1),
+    )
     turned = call(
-        turn_first, (4, M, LANES), 60, late, green, green, mirrors[0], mirror_edge, start, start_edge,
-        zero, scalars=1, blocks=green_blocks(0),
-    )
-    turned_up = call(
-        turn_second, (4, M, LANES), 60, late, green, green, *mirrors, start, zero,
-        scalars=1, blocks=green_blocks(1),
+        turn_second, (5, M, LANES), 60, late, green, green, *mirrors, mirror_edge, start,
+        start_edge, zero, scalars=1, blocks=green_blocks(16, 0),
     )
     by_rows = exchange(along_z, "row").reshape(1024, LANES)
     along_y = call(y_forward, (32, 8, 8, LANES), 16, by_rows, forward, scratch=[pltpu.VMEM((2 * M, LANES), jnp.float32)])
     by_cols = exchange(along_y.reshape(32, HALF, LANES), "col").reshape(2048, LANES)
-    back_x = call(x_both, (2048, LANES), 24, by_cols, turned, turned_up, forward, backward)
+    back_x = call(x_both, (2048, LANES), 24, by_cols, turned_up, turned, forward, backward)
     by_cells = exchange(back_x.reshape(32, HALF, LANES), "col")
     back_y = call(
         y_backward, (1024, LANES), 16, by_cells.reshape(32, 8, 8, LANES), backward,

time: 197 us -> 197 us (level)
    ppermute x3, waiting for transfers between devices: 10.3 us -> 12.2 us  [reflect(): return lax.ppermute(value, ('row', 'col'), pairs)]
  transfers between devices with their start and end apart: 11 -> 11, of which waited for: 7 -> 6; matrix products, arithmetic and copies ran while one was open for 3% -> 3% of each run, Pallas kernels for 5% -> 4%
where the time goes in v6:
time: 197 us; the launch traced here: 195 us
  waiting for transfers between devices  68.1 us (35%)
  blocking collectives  65.9 us (33%)
  starting transfers between devices  34.6 us (18%)
  Pallas kernels  17.1 us (9%)
  local copies, waits for them, and re-layouts  8.86 us (4%)
    all_to_all x3, blocking collectives, exchange(): return lax.all_to_all(value, axis, split_axis=0, concat_axis=0, tiled=True)  65.9 us
    ppermute x4, waiting for transfers between devices, on_device(): half = lax.ppermute(half, *moves[name])  53 us
    pallas_call x7, Pallas kernels, call(): pl.pallas_call(body, out_shape=jax.ShapeDtypeStruct(shape, jnp.float32),...  17.1 us
    all_to_all x1, starting transfers between devices, exchange(): return lax.all_to_all(value, axis, split_axis=0, concat_axis=0, tiled=True)  12.8 us
    ppermute x3, waiting for transfers between devices, reflect(): return lax.ppermute(value, ('row', 'col'), pairs)  12.2 us
    ppermute x4, starting transfers between devices, on_device(): half = lax.ppermute(half, *moves[name])  8.96 us
    ppermute x3, starting transfers between devices, reflect(): return lax.ppermute(value, ('row', 'col'), pairs)  6.98 us
    ppermute x3, starting transfers between devices, spread(): value = value + lax.ppermute(value, 'row', pairs)  5.87 us
  transfers between devices with their start and end apart: 11, of which 6 were waited for; matrix products, arithmetic and copies ran while one was open for 3% of the time, Pallas kernels for 4%

profile of v6, /device:TPU:1, one launch (start us, length us, event | category | flops | bytes accessed | tf_op | source)
XLA Modules:
  0.0 195.4 jit_solution(13301283990186910326)
XLA Ops:
  0.0 0.0 copy-start.3
  0.0 2.6 %shard_map.55 = f32[8,128,128]{2,1,0:T(8,128)} custom-call(f32[256,256]{1,0:T(8,128)} %bitcast.21, bf16[2,512,256]{2,1,0:T(8,128)(2,1)} %constant.18.clone.table), custom_call_target="tpu_custom_call" | custom-call | flops 1000000000 | bytes 524288 | tf_op jit(solution)/shard_map/pallas_call | solution.py:229
  2.6 15.1 %all_to_all.20 = f32[8,128,128]{2,1,0:T(8,128)S(1)} all-to-all(f32[8,128,128]{2,1,0:T(8,128)} %shard_map.55), channel_id=1, replica_groups=mesh['row'=8,'col'=32] {'row'}, dimensions={0} | all-to-all | bytes 1048576 | tf_op jit(solution)/shard_map/all_to_all | solution.py:251
  17.7 0.0 copy-done.3
  17.7 1.9 shard_map.56
  19.6 12.8 %all-to-all-start.1 = ((f32[32,64,128]{2,1,0:T(8,128)}), f32[32,64,128]{2,1,0:T(8,128)S(1)}, u32[]{:S(2)}, u32[]{:S(2)}) async-start(f32[32,64,128]{2,1,0:T(8,128)} %bitcast.2), calls=%async_computation.1 | async-start | bytes 2097152 | tf_op jit(solution)/shard_map/all_to_all | solution.py:251
  32.3 1.1 slice.16
  33.4 3.0 %collective-permute-start = (f32[32,8,512]{2,1,0:T(8,128)S(1)}, f32[32,8,512]{2,1,0:T(8,128)S(1)}, u32[]{:S(2)}, u32[]{:S(2)}) collective-permute-start(f32[32,8,512]{2,1,0:T(8,128)S(1)} %slice.16), channel_id=1, source_target_pairs={{0,29},{1,28},{2,31},{3,30},{4,25},{5,24},{6,27},{7,26},{8,21},{9,... | collective-permute-start | bytes 1572872 | tf_op jit(solution)/shard_map/ppermute | solution.py:283
  36.4 1.1 slice.19
  37.5 2.8 %collective-permute-start.7 = (f32[32,8,512]{2,1,0:T(8,128)S(1)}, f32[32,8,512]{2,1,0:T(8,128)}, u32[]{:S(2)}, u32[]{:S(2)}) collective-permute-start(f32[32,8,512]{2,1,0:T(8,128)S(1)} %slice.19), channel_id=1, source_target_pairs={{0,226},{1,227},{2,224},{3,225},{4,230},{5,231},{6,228},{7,229},{8... | collective-permute-start | bytes 1572872 | tf_op jit(solution)/shard_map/ppermute | solution.py:283
  40.3 53.0 %collective-permute-done = f32[32,8,512]{2,1,0:T(8,128)S(1)} collective-permute-done((f32[32,8,512]{2,1,0:T(8,128)S(1)}, f32[32,8,512]{2,1,0:T(8,128)S(1)}, u32[]{:S(2)}, u32[]{:S(2)}) %collective-permute-start) | collective-permute-done | bytes 524320 | tf_op jit(solution)/shard_map/ppermute | solution.py:283
  93.3 2.7 %collective-permute-start.1 = (f32[32,8,512]{2,1,0:T(8,128)S(1)}, f32[32,8,512]{2,1,0:T(8,128)S(1)}, u32[]{:S(2)}, u32[]{:S(2)}) collective-permute-start(f32[32,8,512]{2,1,0:T(8,128)S(1)} %collective-permute-done), channel_id=1, source_target_pairs={{0,226},{1,227},{2,224},{3,225},{4,230},{5,231},{6,228},{7,229},{8... | collective-permute-start | bytes 1572872 | tf_op jit(solution)/shard_map/ppermute | solution.py:283
  96.0 0.0 collective-permute-done.7
  96.0 0.5 collective-permute-start.8
  96.4 0.8 slice_bitcast_fusion
  97.2 2.2 %collective-permute-start.2 = (f32[16,512]{1,0:T(8,128)S(1)}, f32[16,512]{1,0:T(8,128)S(1)}, u32[]{:S(2)}, u32[]{:S(2)}) collective-permute-start(f32[16,512]{1,0:T(8,128)S(1)} %slice_bitcast_fusion), channel_id=1, source_target_pairs={{0,31},{1,30},{2,29},{3,28},{4,27},{5,26},{6,25},{7,24},{8,23},{9,... | collective-permute-start | bytes 98312 | tf_op jit(solution)/shard_map/ppermute | solution.py:260
  99.4 0.7 slice.18
  100.1 4.8 %collective-permute-start.3 = (f32[8,512]{1,0:T(8,128)S(1)}, f32[8,512]{1,0:T(8,128)S(1)}, u32[]{:S(2)}, u32[]{:S(2)}) collective-permute-start(f32[8,512]{1,0:T(8,128)S(1)} %broadcast_in_dim.16), channel_id=1, source_target_pairs={{0,0},{1,31},{2,30},{3,29},{4,28},{5,27},{6,26},{7,25},{8,24},{9,2... | collective-permute-start | bytes 49160 | tf_op jit(solution)/shard_map/ppermute | solution.py:260
  104.9 7.7 %collective-permute-done.3.start_edge = f32[8,512]{1,0:T(8,128)S(1)} collective-permute-done((f32[8,512]{1,0:T(8,128)S(1)}, f32[8,512]{1,0:T(8,128)S(1)}, u32[]{:S(2)}, u32[]{:S(2)}) %collective-permute-start.3) | collective-permute-done | bytes 16416 | tf_op jit(solution)/shard_map/ppermute | solution.py:260
  112.7 0.0 copy-start.9
  112.7 0.4 collective-permute-done.2.start
  113.0 0.0 copy-start.7
  113.1 3.3 %collective-permute-start.4 = (f32[40,512]{1,0:T(8,128)S(1)}, f32[40,512]{1,0:T(8,128)S(1)}, u32[]{:S(2)}, u32[]{:S(2)}) collective-permute-start(f32[40,512]{1,0:T(8,128)S(1)} %maximum_select_fusion), channel_id=1, source_target_pairs={{0,128},{1,129},{2,130},{3,131},{4,132},{5,133},{6,134},{7,135},{8... | collective-permute-start | bytes 245768 | tf_op jit(solution)/shard_map/ppermute | solution.py:267
  116.3 1.5 collective-permute-done.4
  117.8 1.3 collective-permute-start.5
  119.1 1.5 collective-permute-done.5
  120.6 1.3 collective-permute-start.6
  121.9 1.1 slice.20
  123.0 0.6 copy.9
  123.6 0.0 collective-permute-start.9
  123.6 0.0 collective-permute-done.6
  123.6 0.6 add.15.zero
  124.3 0.0 collective-permute-done.1.low
  124.3 0.0 copy-start.5
  124.3 0.0 copy-done.7
  124.3 0.8 copy-done.5
  125.1 3.2 %shard_map.57.turned_up = f32[3,512,128]{2,1,0:T(8,128)} custom-call(s32[1]{0:T(128)} %bitcast.4.late, f32[64,16,512]{2,1,0:T(8,128)} %middle.3, f32[64,16,512]{2,1,0:T(8,128)} %middle.3, f32[32,8,512]{2,1,0:T(8,128)} %copy-done.5, f32[16,512]{1,0:T(8,128)} %copy-done.7, f32[40,512]{1,0:T(8,128)} %add.15.zero), custom_call_target="tpu_custom_call" | custom-call | flops 1000000000 | bytes 786432 | tf_op jit(solution)/shard_map/pallas_call | solution.py:229
  128.3 0.0 copy-done.9
  128.3 0.0 copy-start.1
  128.3 0.0 copy-start.2
  128.3 4.1 %collective-permute-done.9.mirror_edge = f32[32,512]{1,0:T(8,128)S(1)} collective-permute-done((f32[32,512]{1,0:T(8,128)}, f32[32,512]{1,0:T(8,128)S(1)}, u32[]{:S(2)}, u32[]{:S(2)}) %collective-permute-start.9) | collective-permute-done | bytes 65568 | tf_op jit(solution)/shard_map/ppermute | solution.py:260
  132.4 0.0 copy-start.8
  132.4 0.0 collective-permute-done.8.high
  132.4 0.6 copy-done.8
  133.0 0.0 copy-start.6
  133.0 0.8 copy-done.6
  133.8 4.1 %shard_map.58.turned = f32[5,512,128]{2,1,0:T(8,128)} custom-call(s32[1]{0:T(128)} %bitcast.4.late, f32[64,16,512]{2,1,0:T(8,128)} %middle.3, f32[64,16,512]{2,1,0:T(8,128)} %middle.3, f32[32,8,512]{2,1,0:T(8,128)} %copy-done.5, f32[32,8,512]{2,1,0:T(8,128)} %copy-done.6, f32[32,512]{1,0:T(8,128)} %copy-done.8, f32[16,512]{1,0:T(8,128)} %copy-done.7, ...), custom_call_target="tpu_custom_call" | custom-call | flops 1000000000 | bytes 1310720 | tf_op jit(solution)/shard_map/pallas_call | solution.py:229
  137.9 0.0 all-to-all-done.1
  137.9 0.0 copy-done.1
  137.9 0.0 copy-done.2
  137.9 0.0 copy-start
  137.9 1.3 copy-done
  139.2 2.9 %shard_map.59 = f32[2048,128]{1,0:T(8,128)S(1)} custom-call(f32[2048,128]{1,0:T(8,128)S(1)} %bitcast.15, f32[3,512,128]{2,1,0:T(8,128)S(1)} %copy-done.1, f32[5,512,128]{2,1,0:T(8,128)S(1)} %copy-done, bf16[2,2,256,256]{3,2,1,0:T(8,128)(2,1)S(1)} %copy-done.3, bf16[2,2,256,256]{3,2,1,0:T(8,128)(2,1)S(1)} %copy-done.2), custom_call_target="tpu_custom_call" | custom-call | flops 1000000000 | bytes 1048576 | tf_op jit(solution)/shard_map/pallas_call | solution.py:229
  142.1 36.9 %all_to_all.21 = f32[32,64,128]{2,1,0:T(8,128)S(1)} all-to-all(f32[32,64,128]{2,1,0:T(8,128)S(1)} %bitcast.16), channel_id=1, replica_groups=mesh['row'=8,'col'=32] {'col'}, dimensions={0} | all-to-all | bytes 2097152 | tf_op jit(solution)/shard_map/all_to_all | solution.py:251
  179.0 0.0 copy-start.4
  179.0 1.0 shard_map.60
  180.1 13.9 %all_to_all.22.data = f32[8,128,128]{2,1,0:T(8,128)S(1)} all-to-all(f32[8,128,128]{2,1,0:T(8,128)S(1)} %bitcast.18), channel_id=1, replica_groups=mesh['row'=8,'col'=32] {'row'}, dimensions={0} | all-to-all | bytes 1048576 | tf_op jit(solution)/shard_map/all_to_all | solution.py:251
  194.0 0.0 copy-done.4
  194.0 1.3 shard_map.61
  (4 shorter events, 0.0 us)
Async XLA Ops:
  0.0 17.7 %copy-start.3 = (bf16[2,2,256,256]{3,2,1,0:T(8,128)(2,1)S(1)}, bf16[2,2,256,256]{3,2,1,0:T(8,128)(2,1)}, u32[]{:S(2)}) copy-start(bf16[2,2,256,256]{3,2,1,0:T(8,128)(2,1)} %constant.19.clone.table.forward) | copy-start | bytes 1572868
  19.6 118.3 %all-to-all-start.1 = ((f32[32,64,128]{2,1,0:T(8,128)}), f32[32,64,128]{2,1,0:T(8,128)S(1)}, u32[]{:S(2)}, u32[]{:S(2)}) async-start(f32[32,64,128]{2,1,0:T(8,128)} %bitcast.2), calls=%async_computation.1 | async-start | bytes 2097152 | tf_op jit(solution)/shard_map/all_to_all | solution.py:251
  33.4 59.8 %collective-permute-start = (f32[32,8,512]{2,1,0:T(8,128)S(1)}, f32[32,8,512]{2,1,0:T(8,128)S(1)}, u32[]{:S(2)}, u32[]{:S(2)}) collective-permute-start(f32[32,8,512]{2,1,0:T(8,128)S(1)} %slice.16), channel_id=1, source_target_pairs={{0,29},{1,28},{2,31},{3,30},{4,25},{5,24},{6,27},{7,26},{8,21},{9,... | collective-permute-start | bytes 1572872 | tf_op jit(solution)/shard_map/ppermute | solution.py:283
  37.5 58.5 %collective-permute-start.7 = (f32[32,8,512]{2,1,0:T(8,128)S(1)}, f32[32,8,512]{2,1,0:T(8,128)}, u32[]{:S(2)}, u32[]{:S(2)}) collective-permute-start(f32[32,8,512]{2,1,0:T(8,128)S(1)} %slice.19), channel_id=1, source_target_pairs={{0,226},{1,227},{2,224},{3,225},{4,230},{5,231},{6,228},{7,229},{8... | collective-permute-start | bytes 1572872 | tf_op jit(solution)/shard_map/ppermute | solution.py:283
  93.3 31.0 %collective-permute-start.1 = (f32[32,8,512]{2,1,0:T(8,128)S(1)}, f32[32,8,512]{2,1,0:T(8,128)S(1)}, u32[]{:S(2)}, u32[]{:S(2)}) collective-permute-start(f32[32,8,512]{2,1,0:T(8,128)S(1)} %collective-permute-done), channel_id=1, source_target_pairs={{0,226},{1,227},{2,224},{3,225},{4,230},{5,231},{6,228},{7,229},{8... | collective-permute-start | bytes 1572872 | tf_op jit(solution)/shard_map/ppermute | solution.py:283
  96.0 36.4 %collective-permute-start.8 = (f32[32,8,512]{2,1,0:T(8,128)}, f32[32,8,512]{2,1,0:T(8,128)S(1)}, u32[]{:S(2)}, u32[]{:S(2)}) collective-permute-start(f32[32,8,512]{2,1,0:T(8,128)} %collective-permute-done.7), channel_id=1, source_target_pairs={{0,29},{1,28},{2,31},{3,30},{4,25},{5,24},{6,27},{7,26},{8,21},{9,... | collective-permute-start | bytes 1572872 | tf_op jit(solution)/shard_map/ppermute | solution.py:283
  97.2 15.8 %collective-permute-start.2 = (f32[16,512]{1,0:T(8,128)S(1)}, f32[16,512]{1,0:T(8,128)S(1)}, u32[]{:S(2)}, u32[]{:S(2)}) collective-permute-start(f32[16,512]{1,0:T(8,128)S(1)} %slice_bitcast_fusion), channel_id=1, source_target_pairs={{0,31},{1,30},{2,29},{3,28},{4,27},{5,26},{6,25},{7,24},{8,23},{9,... | collective-permute-start | bytes 98312 | tf_op jit(solution)/shard_map/ppermute | solution.py:260
  100.1 12.5 %collective-permute-start.3 = (f32[8,512]{1,0:T(8,128)S(1)}, f32[8,512]{1,0:T(8,128)S(1)}, u32[]{:S(2)}, u32[]{:S(2)}) collective-permute-start(f32[8,512]{1,0:T(8,128)S(1)} %broadcast_in_dim.16), channel_id=1, source_target_pairs={{0,0},{1,31},{2,30},{3,29},{4,28},{5,27},{6,26},{7,25},{8,24},{9,2... | collective-permute-start | bytes 49160 | tf_op jit(solution)/shard_map/ppermute | solution.py:260
  112.7 15.6 %copy-start.9 = (f32[8,512]{1,0:T(8,128)}, f32[8,512]{1,0:T(8,128)S(1)}, u32[]{:S(2)}) copy-start(f32[8,512]{1,0:T(8,128)S(1)} %collective-permute-done.3.start_edge) | copy-start | bytes 49156
  113.0 11.2 %copy-start.7 = (f32[16,512]{1,0:T(8,128)}, f32[16,512]{1,0:T(8,128)S(1)}, u32[]{:S(2)}) copy-start(f32[16,512]{1,0:T(8,128)S(1)} %collective-permute-done.2.start) | copy-start | bytes 98308
  113.1 4.8 %collective-permute-start.4 = (f32[40,512]{1,0:T(8,128)S(1)}, f32[40,512]{1,0:T(8,128)S(1)}, u32[]{:S(2)}, u32[]{:S(2)}) collective-permute-start(f32[40,512]{1,0:T(8,128)S(1)} %maximum_select_fusion), channel_id=1, source_target_pairs={{0,128},{1,129},{2,130},{3,131},{4,132},{5,133},{6,134},{7,135},{8... | collective-permute-start | bytes 245768 | tf_op jit(solution)/shard_map/ppermute | solution.py:267
  117.8 2.8 %collective-permute-start.5 = (f32[40,512]{1,0:T(8,128)S(1)}, f32[40,512]{1,0:T(8,128)S(1)}, u32[]{:S(2)}, u32[]{:S(2)}) collective-permute-start(f32[40,512]{1,0:T(8,128)S(1)} %add.13), channel_id=1, source_target_pairs={{0,64},{128,192},{1,65},{129,193},{2,66},{130,194},{3,67},{131,195... | collective-permute-start | bytes 245768 | tf_op jit(solution)/shard_map/ppermute | solution.py:267
  120.6 3.0 %collective-permute-start.6 = (f32[40,512]{1,0:T(8,128)S(1)}, f32[40,512]{1,0:T(8,128)S(1)}, u32[]{:S(2)}, u32[]{:S(2)}) collective-permute-start(f32[40,512]{1,0:T(8,128)S(1)} %add.14), channel_id=1, source_target_pairs={{0,32},{64,96},{128,160},{192,224},{1,33},{65,97},{129,161},{193,2... | collective-permute-start | bytes 245768 | tf_op jit(solution)/shard_map/ppermute | solution.py:267
  123.6 8.8 %collective-permute-start.9 = (f32[32,512]{1,0:T(8,128)}, f32[32,512]{1,0:T(8,128)S(1)}, u32[]{:S(2)}, u32[]{:S(2)}) collective-permute-start(f32[32,512]{1,0:T(8,128)} %bitcast.14), channel_id=1, source_target_pairs={{0,224},{1,255},{2,254},{3,253},{4,252},{5,251},{6,250},{7,249},{8... | collective-permute-start | bytes 196616 | tf_op jit(solution)/shard_map/ppermute | solution.py:260
  124.3 0.8 copy-start.5
  128.3 9.6 %copy-start.1 = (f32[3,512,128]{2,1,0:T(8,128)S(1)}, f32[3,512,128]{2,1,0:T(8,128)}, u32[]{:S(2)}) copy-start(f32[3,512,128]{2,1,0:T(8,128)} %shard_map.57.turned_up) | copy-start | bytes 2359300
  128.3 9.6 %copy-start.2 = (bf16[2,2,256,256]{3,2,1,0:T(8,128)(2,1)S(1)}, bf16[2,2,256,256]{3,2,1,0:T(8,128)(2,1)}, u32[]{:S(2)}) copy-start(bf16[2,2,256,256]{3,2,1,0:T(8,128)(2,1)} %constant.20.clone.backward) | copy-start | bytes 1572868
  132.4 0.6 copy-start.8
  133.0 0.8 copy-start.6
  137.9 1.3 copy-start
  179.0 15.0 %copy-start.4 = (bf16[2,512,256]{2,1,0:T(8,128)(2,1)S(1)}, bf16[2,512,256]{2,1,0:T(8,128)(2,1)}, u32[]{:S(2)}) copy-start(bf16[2,512,256]{2,1,0:T(8,128)(2,1)} %constant.18.clone.table) | copy-start | bytes 1572868

commit v7 on v6

--- a/solution.py
+++ b/solution.py
@@ -247,6 +247,29 @@
     ]
 
 
+def pack_edges(upper, plane, edge, start, start_edge):
+    edge[...] = upper[:, 0, :]
+    start[...] = plane[0]
+    start_edge[...] = jnp.broadcast_to(plane[0, 0:1, :], (8, M))
+
+
+def packed_edges(green):
+    shapes = [jax.ShapeDtypeStruct((n, M), jnp.float32) for n in (SLOTS, 16, 8)]
+    return pl.pallas_call(
+        pack_edges,
+        out_shape=shapes,
+        grid=(1,),
+        in_specs=[
+            pl.BlockSpec((SLOTS, 8, M), lambda i: (1, 0, 0)),
+            pl.BlockSpec((1, 16, M), lambda i: (0, 0, 0)),
+        ],
+        out_specs=[pl.BlockSpec(memory_space=pltpu.VMEM)] * 3,
+        compiler_params=pltpu.CompilerParams(vmem_limit_bytes=16 * 1024 * 1024),
+        cost_estimate=pl.CostEstimate(flops=10**6, bytes_accessed=10**6, transcendentals=0),
+        name="pack_edges",
+    )(green, green)
+
+
 def exchange(value, axis):
     return lax.all_to_all(value, axis, split_axis=0, concat_axis=0, tiled=True)
 
@@ -282,10 +305,11 @@
         for name in order:
             half = lax.ppermute(half, *moves[name])
         mirrors.append(half)
-    mirror_edge = reflect(green[SLOTS:, 0], 7, 32)
-    start = reflect(green[0], 8, 31)
-    start_edge = reflect(jnp.broadcast_to(green[0, :1], (8, M)), 8, 32)
-    zero = spread(jnp.concatenate([green[0], start, start_edge], 0))
+    edge, plane, corner = packed_edges(green)
+    mirror_edge = reflect(edge, 7, 32)
+    start = reflect(plane, 8, 31)
+    start_edge = reflect(corner, 8, 32)
+    zero = spread(jnp.concatenate([plane, start, start_edge], 0))
     row = lax.axis_index("row")
     late = ((row >= 4).astype(jnp.int32) + (row == 4).astype(jnp.int32))[None]
     turned_up = call(

time: 197 us -> 195 us (0.990)
  local copies, waits for them, and re-layouts: 8.86 us -> 3 us
  waiting for transfers between devices: 68.1 us -> 72.2 us
    ppermute x4, waiting for transfers between devices: 53 us -> 55.1 us  [on_device(): half = lax.ppermute(half, *moves[name])]
    slice x2, local copies, waits for them, and re-layouts: 2.15 us -> 0.08 us  [on_device(): half = (green, later)[k][SLOTS:, 8 * k:8 * (k + 1)]]
    unnamed x21 -> x22, local copies, waits for them, and re-layouts: 4.14 us -> 2.93 us
  transfers between devices with their start and end apart: 11 -> 11, of which waited for: 6 -> 7; matrix products, arithmetic and copies ran while one was open for 3% -> 0% of each run, Pallas kernels for 4% -> 4%
where the time goes in v7:
time: 195 us; the launch traced here: 193 us
  waiting for transfers between devices  72.2 us (37%)
  blocking collectives  65.9 us (34%)
  starting transfers between devices  34.7 us (18%)
  Pallas kernels  16.2 us (8%)
  local copies, waits for them, and re-layouts  3 us (2%)
    all_to_all x3, blocking collectives, exchange(): return lax.all_to_all(value, axis, split_axis=0, concat_axis=0, tiled=True)  65.9 us
    ppermute x4, waiting for transfers between devices, on_device(): half = lax.ppermute(half, *moves[name])  55.1 us
    pallas_call x7, Pallas kernels, call(): pl.pallas_call(body, out_shape=jax.ShapeDtypeStruct(shape, jnp.float32),...  16.1 us
    all_to_all x1, starting transfers between devices, exchange(): return lax.all_to_all(value, axis, split_axis=0, concat_axis=0, tiled=True)  12.8 us
    ppermute x3, waiting for transfers between devices, reflect(): return lax.ppermute(value, ('row', 'col'), pairs)  12.8 us
    ppermute x4, starting transfers between devices, on_device(): half = lax.ppermute(half, *moves[name])  8.95 us
    ppermute x3, starting transfers between devices, reflect(): return lax.ppermute(value, ('row', 'col'), pairs)  7.16 us
    ppermute x3, starting transfers between devices, spread(): value = value + lax.ppermute(value, 'row', pairs)  5.87 us
  transfers between devices with their start and end apart: 11, of which 7 were waited for; matrix products, arithmetic and copies ran while one was open for 0% of the time, Pallas kernels for 4%

profile of v7, /device:TPU:1, one launch (start us, length us, event | category | flops | bytes accessed | tf_op | source)
XLA Modules:
  0.0 192.9 jit_solution(17396688888102040801)
XLA Ops:
  0.0 0.0 copy-start.5
  0.0 2.6 %shard_map.55 = f32[8,128,128]{2,1,0:T(8,128)} custom-call(f32[256,256]{1,0:T(8,128)} %bitcast.15, bf16[2,512,256]{2,1,0:T(8,128)(2,1)} %constant.18.clone.table), custom_call_target="tpu_custom_call" | custom-call | flops 1000000000 | bytes 524288 | tf_op jit(solution)/shard_map/pallas_call | solution.py:229
  2.6 15.1 %all_to_all.20 = f32[8,128,128]{2,1,0:T(8,128)S(1)} all-to-all(f32[8,128,128]{2,1,0:T(8,128)} %shard_map.55), channel_id=1, replica_groups=mesh['row'=8,'col'=32] {'row'}, dimensions={0} | all-to-all | bytes 1048576 | tf_op jit(solution)/shard_map/all_to_all | solution.py:274
  17.7 0.0 copy-done.5
  17.7 0.0 copy-start
  17.7 0.9 shard_map.56
  18.6 0.0 copy-start.3
  18.6 1.0 copy-done.3
  19.6 12.8 %all-to-all-start.1 = ((f32[32,64,128]{2,1,0:T(8,128)}), f32[32,64,128]{2,1,0:T(8,128)S(1)}, u32[]{:S(2)}, u32[]{:S(2)}) async-start(f32[32,64,128]{2,1,0:T(8,128)} %bitcast.11), calls=%async_computation.1 | async-start | bytes 2097152 | tf_op jit(solution)/shard_map/all_to_all | solution.py:274
  32.4 0.0 copy-done
  32.4 3.0 %collective-permute-start = (f32[32,8,512]{2,1,0:T(8,128)S(1)}, f32[32,8,512]{2,1,0:T(8,128)}, u32[]{:S(2)}, u32[]{:S(2)}) collective-permute-start(f32[32,8,512]{2,1,0:T(8,128)S(1)} %slice.6), channel_id=1, source_target_pairs={{0,29},{1,28},{2,31},{3,30},{4,25},{5,24},{6,27},{7,26},{8,21},{9,... | collective-permute-start | bytes 1572872 | tf_op jit(solution)/shard_map/ppermute | solution.py:306
  35.5 2.8 %collective-permute-start.7 = (f32[32,8,512]{2,1,0:T(8,128)S(1)}, f32[32,8,512]{2,1,0:T(8,128)}, u32[]{:S(2)}, u32[]{:S(2)}) collective-permute-start(f32[32,8,512]{2,1,0:T(8,128)S(1)} %slice.7), channel_id=1, source_target_pairs={{0,226},{1,227},{2,224},{3,225},{4,230},{5,231},{6,228},{7,229},{8... | collective-permute-start | bytes 1572872 | tf_op jit(solution)/shard_map/ppermute | solution.py:306
  38.3 55.1 %collective-permute-done = f32[32,8,512]{2,1,0:T(8,128)} collective-permute-done((f32[32,8,512]{2,1,0:T(8,128)S(1)}, f32[32,8,512]{2,1,0:T(8,128)}, u32[]{:S(2)}, u32[]{:S(2)}) %collective-permute-start) | collective-permute-done | bytes 524320 | tf_op jit(solution)/shard_map/ppermute | solution.py:306
  93.4 2.7 %collective-permute-start.1 = (f32[32,8,512]{2,1,0:T(8,128)}, f32[32,8,512]{2,1,0:T(8,128)}, u32[]{:S(2)}, u32[]{:S(2)}) collective-permute-start(f32[32,8,512]{2,1,0:T(8,128)} %collective-permute-done), channel_id=1, source_target_pairs={{0,226},{1,227},{2,224},{3,225},{4,230},{5,231},{6,228},{7,229},{8... | collective-permute-start | bytes 1572872 | tf_op jit(solution)/shard_map/ppermute | solution.py:306
  96.1 0.0 collective-permute-done.7
  96.1 0.5 collective-permute-start.8
  96.6 0.1 pack_edges.1
  96.6 2.3 %collective-permute-start.2 = (f32[16,512]{1,0:T(8,128)S(1)}, f32[16,512]{1,0:T(8,128)S(1)}, u32[]{:S(2)}, u32[]{:S(2)}) collective-permute-start(f32[16,512]{1,0:T(8,128)S(1)} %get-tuple-element.11), channel_id=1, source_target_pairs={{0,31},{1,30},{2,29},{3,28},{4,27},{5,26},{6,25},{7,24},{8,23},{9,... | collective-permute-start | bytes 98312 | tf_op jit(solution)/shard_map/ppermute | solution.py:283
  98.9 4.8 %collective-permute-start.3 = (f32[8,512]{1,0:T(8,128)S(1)}, f32[8,512]{1,0:T(8,128)S(1)}, u32[]{:S(2)}, u32[]{:S(2)}) collective-permute-start(f32[8,512]{1,0:T(8,128)S(1)} %get-tuple-element.12), channel_id=1, source_target_pairs={{0,0},{1,31},{2,30},{3,29},{4,28},{5,27},{6,26},{7,25},{8,24},{9,2... | collective-permute-start | bytes 49160 | tf_op jit(solution)/shard_map/ppermute | solution.py:283
  103.7 9.1 %collective-permute-done.3.start_edge = f32[8,512]{1,0:T(8,128)S(1)} collective-permute-done((f32[8,512]{1,0:T(8,128)S(1)}, f32[8,512]{1,0:T(8,128)S(1)}, u32[]{:S(2)}, u32[]{:S(2)}) %collective-permute-start.3) | collective-permute-done | bytes 16416 | tf_op jit(solution)/shard_map/ppermute | solution.py:283
  112.8 0.0 copy-start.10
  112.8 0.4 collective-permute-done.2.start
  113.2 0.0 copy-start.8
  113.2 3.3 %collective-permute-start.4 = (f32[40,512]{1,0:T(8,128)S(1)}, f32[40,512]{1,0:T(8,128)S(1)}, u32[]{:S(2)}, u32[]{:S(2)}) collective-permute-start(f32[40,512]{1,0:T(8,128)S(1)} %maximum_select_fusion), channel_id=1, source_target_pairs={{0,128},{1,129},{2,130},{3,131},{4,132},{5,133},{6,134},{7,135},{8... | collective-permute-start | bytes 245768 | tf_op jit(solution)/shard_map/ppermute | solution.py:290
  116.5 1.5 collective-permute-done.4
  118.0 1.3 collective-permute-start.5
  119.3 1.5 collective-permute-done.5
  120.7 1.3 collective-permute-start.6
  122.0 0.1 collective-permute-start.9
  122.2 1.4 collective-permute-done.6
  123.5 0.6 add.15.zero
  124.2 0.0 collective-permute-done.1.low
  124.2 0.0 copy-done.8
  124.2 3.2 %shard_map.57.turned_up = f32[3,512,128]{2,1,0:T(8,128)} custom-call(s32[1]{0:T(128)} %bitcast.4.late, f32[64,16,512]{2,1,0:T(8,128)} %middle.3, f32[64,16,512]{2,1,0:T(8,128)} %middle.3, f32[32,8,512]{2,1,0:T(8,128)} %collective-permute-done.1.low, f32[16,512]{1,0:T(8,128)} %copy-done.8, f32[40,512]{1,0:T(8,128)} %add.15.zero), custom_call_target="tpu_custom_call" | custom-call | flops 1000000000 | bytes 786432 | tf_op jit(solution)/shard_map/pallas_call | solution.py:229
  127.4 0.0 copy-done.10
  127.4 0.0 copy-start.2
  127.4 0.0 copy-start.4
  127.4 0.0 copy-start.6
  127.4 3.3 %collective-permute-done.9.mirror_edge = f32[32,512]{1,0:T(8,128)S(1)} collective-permute-done((f32[32,512]{1,0:T(8,128)S(1)}, f32[32,512]{1,0:T(8,128)S(1)}, u32[]{:S(2)}, u32[]{:S(2)}) %collective-permute-start.9) | collective-permute-done | bytes 65568 | tf_op jit(solution)/shard_map/ppermute | solution.py:283
  130.7 0.0 copy-start.9
  130.7 0.0 collective-permute-done.8.high
  130.7 0.6 copy-done.9
  131.3 4.1 %shard_map.58.turned = f32[5,512,128]{2,1,0:T(8,128)} custom-call(s32[1]{0:T(128)} %bitcast.4.late, f32[64,16,512]{2,1,0:T(8,128)} %middle.3, f32[64,16,512]{2,1,0:T(8,128)} %middle.3, f32[32,8,512]{2,1,0:T(8,128)} %collective-permute-done.1.low, f32[32,8,512]{2,1,0:T(8,128)} %collective-permute-done.8.high, f32[32,512]{1,0:T(8,128)} %copy-done.9, ...), custom_call_target="tpu_custom_call" | custom-call | flops 1000000000 | bytes 1310720 | tf_op jit(solution)/shard_map/pallas_call | solution.py:229
  135.4 0.0 all-to-all-done.1
  135.4 0.0 copy-done.2
  135.4 0.0 copy-done.4
  135.4 0.0 copy-done.6
  135.4 0.0 copy-start.1
  135.4 1.3 copy-done.1
  136.7 2.9 %shard_map.59 = f32[2048,128]{1,0:T(8,128)S(1)} custom-call(f32[2048,128]{1,0:T(8,128)S(1)} %bitcast.9, f32[3,512,128]{2,1,0:T(8,128)S(1)} %copy-done.2, f32[5,512,128]{2,1,0:T(8,128)S(1)} %copy-done.1, bf16[2,2,256,256]{3,2,1,0:T(8,128)(2,1)S(1)} %copy-done.6, bf16[2,2,256,256]{3,2,1,0:T(8,128)(2,1)S(1)} %copy-done.4), custom_call_target="tpu_custom_call" | custom-call | flops 1000000000 | bytes 1048576 | tf_op jit(solution)/shard_map/pallas_call | solution.py:229
  139.7 36.9 %all_to_all.21 = f32[32,64,128]{2,1,0:T(8,128)S(1)} all-to-all(f32[32,64,128]{2,1,0:T(8,128)S(1)} %bitcast.10), channel_id=1, replica_groups=mesh['row'=8,'col'=32] {'col'}, dimensions={0} | all-to-all | bytes 2097152 | tf_op jit(solution)/shard_map/all_to_all | solution.py:274
  176.6 0.0 copy-start.7
  176.6 1.0 shard_map.60
  177.6 13.9 %all_to_all.22.data = f32[8,128,128]{2,1,0:T(8,128)S(1)} all-to-all(f32[8,128,128]{2,1,0:T(8,128)S(1)} %bitcast.13), channel_id=1, replica_groups=mesh['row'=8,'col'=32] {'row'}, dimensions={0} | all-to-all | bytes 1048576 | tf_op jit(solution)/shard_map/all_to_all | solution.py:274
  191.6 0.0 copy-done.7
  191.6 1.3 shard_map.61
  (5 shorter events, 0.1 us)
Async XLA Ops:
  0.0 17.7 %copy-start.5 = (bf16[2,2,256,256]{3,2,1,0:T(8,128)(2,1)S(1)}, bf16[2,2,256,256]{3,2,1,0:T(8,128)(2,1)}, u32[]{:S(2)}) copy-start(bf16[2,2,256,256]{3,2,1,0:T(8,128)(2,1)} %constant.19.clone.table.forward) | copy-start | bytes 1572868
  17.7 14.7 %copy-start = (f32[64,16,512]{2,1,0:T(8,128)S(1)}, f32[64,16,512]{2,1,0:T(8,128)}, u32[]{:S(2)}) copy-start(f32[64,16,512]{2,1,0:T(8,128)} %middle.3) | copy-start | bytes 6291460
  18.6 1.0 copy-start.3
  19.6 115.8 %all-to-all-start.1 = ((f32[32,64,128]{2,1,0:T(8,128)}), f32[32,64,128]{2,1,0:T(8,128)S(1)}, u32[]{:S(2)}, u32[]{:S(2)}) async-start(f32[32,64,128]{2,1,0:T(8,128)} %bitcast.11), calls=%async_computation.1 | async-start | bytes 2097152 | tf_op jit(solution)/shard_map/all_to_all | solution.py:274
  32.4 61.0 %collective-permute-start = (f32[32,8,512]{2,1,0:T(8,128)S(1)}, f32[32,8,512]{2,1,0:T(8,128)}, u32[]{:S(2)}, u32[]{:S(2)}) collective-permute-start(f32[32,8,512]{2,1,0:T(8,128)S(1)} %slice.6), channel_id=1, source_target_pairs={{0,29},{1,28},{2,31},{3,30},{4,25},{5,24},{6,27},{7,26},{8,21},{9,... | collective-permute-start | bytes 1572872 | tf_op jit(solution)/shard_map/ppermute | solution.py:306
  35.5 60.6 %collective-permute-start.7 = (f32[32,8,512]{2,1,0:T(8,128)S(1)}, f32[32,8,512]{2,1,0:T(8,128)}, u32[]{:S(2)}, u32[]{:S(2)}) collective-permute-start(f32[32,8,512]{2,1,0:T(8,128)S(1)} %slice.7), channel_id=1, source_target_pairs={{0,226},{1,227},{2,224},{3,225},{4,230},{5,231},{6,228},{7,229},{8... | collective-permute-start | bytes 1572872 | tf_op jit(solution)/shard_map/ppermute | solution.py:306
  93.4 30.8 %collective-permute-start.1 = (f32[32,8,512]{2,1,0:T(8,128)}, f32[32,8,512]{2,1,0:T(8,128)}, u32[]{:S(2)}, u32[]{:S(2)}) collective-permute-start(f32[32,8,512]{2,1,0:T(8,128)} %collective-permute-done), channel_id=1, source_target_pairs={{0,226},{1,227},{2,224},{3,225},{4,230},{5,231},{6,228},{7,229},{8... | collective-permute-start | bytes 1572872 | tf_op jit(solution)/shard_map/ppermute | solution.py:306
  96.1 34.6 %collective-permute-start.8 = (f32[32,8,512]{2,1,0:T(8,128)}, f32[32,8,512]{2,1,0:T(8,128)}, u32[]{:S(2)}, u32[]{:S(2)}) collective-permute-start(f32[32,8,512]{2,1,0:T(8,128)} %collective-permute-done.7), channel_id=1, source_target_pairs={{0,29},{1,28},{2,31},{3,30},{4,25},{5,24},{6,27},{7,26},{8,21},{9,... | collective-permute-start | bytes 1572872 | tf_op jit(solution)/shard_map/ppermute | solution.py:306
  96.6 16.6 %collective-permute-start.2 = (f32[16,512]{1,0:T(8,128)S(1)}, f32[16,512]{1,0:T(8,128)S(1)}, u32[]{:S(2)}, u32[]{:S(2)}) collective-permute-start(f32[16,512]{1,0:T(8,128)S(1)} %get-tuple-element.11), channel_id=1, source_target_pairs={{0,31},{1,30},{2,29},{3,28},{4,27},{5,26},{6,25},{7,24},{8,23},{9,... | collective-permute-start | bytes 98312 | tf_op jit(solution)/shard_map/ppermute | solution.py:283
  98.9 13.9 %collective-permute-start.3 = (f32[8,512]{1,0:T(8,128)S(1)}, f32[8,512]{1,0:T(8,128)S(1)}, u32[]{:S(2)}, u32[]{:S(2)}) collective-permute-start(f32[8,512]{1,0:T(8,128)S(1)} %get-tuple-element.12), channel_id=1, source_target_pairs={{0,0},{1,31},{2,30},{3,29},{4,28},{5,27},{6,26},{7,25},{8,24},{9,2... | collective-permute-start | bytes 49160 | tf_op jit(solution)/shard_map/ppermute | solution.py:283
  112.8 14.6 %copy-start.10 = (f32[8,512]{1,0:T(8,128)}, f32[8,512]{1,0:T(8,128)S(1)}, u32[]{:S(2)}) copy-start(f32[8,512]{1,0:T(8,128)S(1)} %collective-permute-done.3.start_edge) | copy-start | bytes 49156
  113.2 11.0 %copy-start.8 = (f32[16,512]{1,0:T(8,128)}, f32[16,512]{1,0:T(8,128)S(1)}, u32[]{:S(2)}) copy-start(f32[16,512]{1,0:T(8,128)S(1)} %collective-permute-done.2.start) | copy-start | bytes 98308
  113.2 4.8 %collective-permute-start.4 = (f32[40,512]{1,0:T(8,128)S(1)}, f32[40,512]{1,0:T(8,128)S(1)}, u32[]{:S(2)}, u32[]{:S(2)}) collective-permute-start(f32[40,512]{1,0:T(8,128)S(1)} %maximum_select_fusion), channel_id=1, source_target_pairs={{0,128},{1,129},{2,130},{3,131},{4,132},{5,133},{6,134},{7,135},{8... | collective-permute-start | bytes 245768 | tf_op jit(solution)/shard_map/ppermute | solution.py:290
  118.0 2.8 %collective-permute-start.5 = (f32[40,512]{1,0:T(8,128)S(1)}, f32[40,512]{1,0:T(8,128)S(1)}, u32[]{:S(2)}, u32[]{:S(2)}) collective-permute-start(f32[40,512]{1,0:T(8,128)S(1)} %add.13), channel_id=1, source_target_pairs={{0,64},{128,192},{1,65},{129,193},{2,66},{130,194},{3,67},{131,195... | collective-permute-start | bytes 245768 | tf_op jit(solution)/shard_map/ppermute | solution.py:290
  120.7 2.8 %collective-permute-start.6 = (f32[40,512]{1,0:T(8,128)S(1)}, f32[40,512]{1,0:T(8,128)S(1)}, u32[]{:S(2)}, u32[]{:S(2)}) collective-permute-start(f32[40,512]{1,0:T(8,128)S(1)} %add.14), channel_id=1, source_target_pairs={{0,32},{64,96},{128,160},{192,224},{1,33},{65,97},{129,161},{193,2... | collective-permute-start | bytes 245768 | tf_op jit(solution)/shard_map/ppermute | solution.py:290
  122.0 8.6 %collective-permute-start.9 = (f32[32,512]{1,0:T(8,128)S(1)}, f32[32,512]{1,0:T(8,128)S(1)}, u32[]{:S(2)}, u32[]{:S(2)}) collective-permute-start(f32[32,512]{1,0:T(8,128)S(1)} %get-tuple-element.14), channel_id=1, source_target_pairs={{0,224},{1,255},{2,254},{3,253},{4,252},{5,251},{6,250},{7,249},{8... | collective-permute-start | bytes 196616 | tf_op jit(solution)/shard_map/ppermute | solution.py:283
  127.4 8.0 %copy-start.2 = (f32[3,512,128]{2,1,0:T(8,128)S(1)}, f32[3,512,128]{2,1,0:T(8,128)}, u32[]{:S(2)}) copy-start(f32[3,512,128]{2,1,0:T(8,128)} %shard_map.57.turned_up) | copy-start | bytes 2359300
  127.4 8.0 %copy-start.4 = (bf16[2,2,256,256]{3,2,1,0:T(8,128)(2,1)S(1)}, bf16[2,2,256,256]{3,2,1,0:T(8,128)(2,1)}, u32[]{:S(2)}) copy-start(bf16[2,2,256,256]{3,2,1,0:T(8,128)(2,1)} %constant.20.clone.backward) | copy-start | bytes 1572868
  127.4 8.0 %copy-start.6 = (bf16[2,2,256,256]{3,2,1,0:T(8,128)(2,1)S(1)}, bf16[2,2,256,256]{3,2,1,0:T(8,128)(2,1)}, u32[]{:S(2)}) copy-start(bf16[2,2,256,256]{3,2,1,0:T(8,128)(2,1)} %constant.19.clone.table.forward) | copy-start | bytes 1572868
  130.7 0.6 copy-start.9
  135.4 1.3 copy-start.1
  176.6 15.0 %copy-start.7 = (bf16[2,512,256]{2,1,0:T(8,128)(2,1)S(1)}, bf16[2,512,256]{2,1,0:T(8,128)(2,1)}, u32[]{:S(2)}) copy-start(bf16[2,512,256]{2,1,0:T(8,128)(2,1)} %constant.18.clone.table) | copy-start | bytes 1572868
